TPU v7x, 32 devices: a whole 2x2x4 slice. The times are simulated.
32 devices in a mesh: section: 16 (over z, x, core), dp: 2 (over y).
Axes of the slice: x: 2, y: 2, z: 4, core: 2. Of those that a mesh axis runs over, the one named last changes fastest.
Arguments:
- cotangent: bfloat16 [128, 8192], P('dp'), may hold values from -96 to 96
- lengths: int32 [4], P('dp'), may hold values from 1 to 32, as said below
- example_ids: int32 [128], P('dp'), may hold values from -1 to 3, as said below
- layer_inputs: bfloat16 [128, 32768], P('dp', 'section'), may hold values from -6 to 6
- preacts: bfloat16 [128, 32768], P('dp', 'section'), may hold values from -6 to 6
- weights: bfloat16 [32768, 8192], P('section', 'dp'), may hold values from -0.0625 to 0.0625
- query_left: bfloat16 [32768, 256], P('section'), may hold values from -0.0625 to 0.0625
- query_right: bfloat16 [32768, 256], P('section'), may hold values from -0.0625 to 0.0625
Outputs:
- input_grads: bfloat16 [128, 32768], P('dp', 'section')
- scores: float32 [4, 16], P('dp')
Inputs may be any that keep to these rules, and one draw needn't show every extreme that they name: In each aligned block of 2 sequences one length is exactly 32; the lengths of a block sum to at most 64. `example_ids`: rows n * 64 to (n + 1) * 64 - 1 hold sequences n * 2 to (n + 1) * 2 - 1 in order from the block's first row, each on as many consecutive rows as its length; the block's remaining rows hold -1.
All inputs are finite; a program needn't handle non-finite values.
Results may differ from a plain program's by a relative error of at most 0.0066.
Values may be sent and summed in bfloat16 or wider, within the bound.
No kernel may reach another device: no remote copies, remote signals or barrier semaphores. Data moves between devices by JAX's collectives and lax.ppermute only.
A program may use at most 64 MiB of HBM per device.

v0:
```python
import jax
import jax.numpy as jnp
from jax import lax
from jax.sharding import PartitionSpec as P

LAYERS = 4
QUERIES = 16
RANK = 16
ROWS = 32


def from_partner(value, axis, distance):
    mask = 2**distance
    pairs = [(source, source ^ mask) for source in range(lax.axis_size(axis))]
    return lax.ppermute(value, axis, pairs)


def from_behind(value, axis, steps):
    count = lax.axis_size(axis)
    first, last = (max(0, -steps), min(count, count - steps))
    return lax.ppermute(value, axis, [(source, source + steps) for source in range(first, last)])


def silu_slope(preact):
    sigmoid_value = jax.nn.sigmoid(preact)
    return sigmoid_value * (1.0 + preact * (1.0 - sigmoid_value))


def per_device(
    cotangent, lengths, example_ids, layer_inputs, preacts, weights, query_left, query_right
):
    per_section = lax.axis_size("section") // LAYERS
    level_count = per_section.bit_length() - 1
    position = lax.axis_index("section")
    section_index = position // per_section
    column_block = position % per_section
    group_index = lax.axis_index("dp")
    token_count = cotangent.shape[0]
    block_cols = layer_inputs.shape[1]
    seq_count = lengths.shape[0]
    micro_count = token_count // ROWS
    step_count = LAYERS + micro_count - 1
    seq_slots = group_index * seq_count + jnp.arange(seq_count, dtype=jnp.int32)
    member = (example_ids[:, None] == seq_slots[None, :]).astype(jnp.float32)
    token_len = jnp.dot(member, lengths.astype(jnp.float32), precision=lax.Precision.HIGHEST)
    token_scale = jnp.where(example_ids >= 0, 1.0 / jnp.maximum(token_len, 1.0), 0.0)
    top_columns = lax.dynamic_slice_in_dim(cotangent, column_block * block_cols, block_cols, 1)
    top_grad = (top_columns.astype(jnp.float32) * token_scale[:, None]).astype(jnp.bfloat16)
    right_full = query_right
    for level_bit in range(level_count):
        partner = from_partner(right_full, "section", level_bit)
        upper_half = column_block >> level_bit & 1
        right_full = jnp.where(
            upper_half == 1,
            jnp.concatenate([partner, right_full], 0),
            jnp.concatenate([right_full, partner], 0),
        )

    def gather_gate(gate_grad):
        combined = gate_grad
        for level_bit in range(level_count):
            partner = from_partner(combined, "section", level_bit)
            upper_half = column_block >> level_bit & 1
            combined = jnp.where(
                upper_half == 1,
                jnp.concatenate([partner, combined], 1),
                jnp.concatenate([combined, partner], 1),
            )
        return combined

    def score_terms(gate_full, input_rows, id_rows):
        left_part = jnp.dot(input_rows, query_left, preferred_element_type=jnp.float32)
        right_part = jnp.dot(gate_full, right_full, preferred_element_type=jnp.float32)
        per_token = jnp.sum((left_part * right_part).reshape(ROWS, QUERIES, RANK), axis=2)
        block_member = (id_rows[:, None] == seq_slots[None, :]).astype(jnp.float32)
        return jnp.dot(block_member.T, per_token, precision=lax.Precision.HIGHEST)

    def advance(clock_tick, loop_state):
        outgoing, grad_store, totals = loop_state
        arrived = from_behind(outgoing, "section", -per_section)
        micro_index = clock_tick - (LAYERS - 1 - section_index)
        in_range = (micro_index >= 0) & (micro_index < micro_count)
        row_start = jnp.clip(micro_index, 0, micro_count - 1) * ROWS
        top_rows = lax.dynamic_slice_in_dim(top_grad, row_start, ROWS, 0)
        grad_out = jnp.where(section_index == LAYERS - 1, top_rows, arrived)
        preact = lax.dynamic_slice_in_dim(preacts, row_start, ROWS, 0).astype(jnp.float32)
        gate_grad = (silu_slope(preact) * grad_out.astype(jnp.float32)).astype(jnp.bfloat16)
        gate_full = gather_gate(gate_grad)
        input_rows = lax.dynamic_slice_in_dim(layer_inputs, row_start, ROWS, 0)
        id_rows = lax.dynamic_slice_in_dim(example_ids, row_start, ROWS, 0)
        by_group = lax.all_to_all(gate_full, "dp", split_axis=1, concat_axis=0, tiled=True)
        backward_sum = lax.psum_scatter(
            lax.dot_general(
                by_group, weights, (((1,), (1,)), ((), ())), preferred_element_type=jnp.float32
            ),
            "dp",
            scatter_dimension=0,
            tiled=True,
        )
        increment = score_terms(gate_full, input_rows, id_rows)
        in_grad = (grad_out.astype(jnp.float32) + backward_sum).astype(jnp.bfloat16)
        updated = lax.dynamic_update_slice_in_dim(grad_store, in_grad, row_start, 0)
        grad_store = jnp.where(in_range, updated, grad_store)
        increment = jnp.where(in_range, increment, 0.0)
        totals = totals + lax.psum(increment, "section")
        return (in_grad, grad_store, totals)

    initial = (
        jnp.zeros((ROWS, block_cols), jnp.bfloat16),
        jnp.zeros((token_count, block_cols), jnp.bfloat16),
        jnp.zeros((seq_count, QUERIES), jnp.float32),
    )
    outgoing, grad_store, totals = lax.fori_loop(0, step_count, advance, initial)
    return (grad_store, totals)


def solution(mesh):
    placed = (
        P("dp", None),
        P("dp"),
        P("dp"),
        P("dp", "section"),
        P("dp", "section"),
        P("section", "dp"),
        P("section", None),
        P("section", None),
    )
    return jax.shard_map(
        per_device,
        mesh=mesh,
        in_specs=placed,
        out_specs=(P("dp", "section"), P("dp", None)),
        check_vma=False,
    )
```

profile of v0, /device:TPU:0, one launch (start us, length us, event | category | flops | bytes accessed | tf_op | source)
XLA Modules:
  0.0 443.8 jit_solution(1843948315144772857)
XLA Ops:
  7.2 0.6 collective-permute-start.3
  7.7 2.5 collective-permute-done.3
  10.2 3.4 maximum_select_fusion.6
  13.6 2.8 collective-permute-start.4
  16.6 1.1 multiply_convert_fusion
  17.8 44.9 %collective-permute-done.4 = bf16[4096,256]{1,0:T(8,128)(2,1)} collective-permute-done((bf16[4096,256]{1,0:T(8,128)(2,1)}, bf16[4096,256]{1,0:T(8,128)(2,1)}, u32[]{:S(2)}, u32[]{:S(2)}) %collective-permute-start.4) | collective-permute-done | bytes 2097184 | tf_op jit(solution)/shard_map/ppermute | solution.py:15
  62.7 5.5 %maximum_select_fusion.5 = bf16[8192,256]{1,0:T(8,128)(2,1)} fusion(bf16[4096,256]{1,0:T(8,128)(2,1)} %maximum_select_fusion.6, bf16[4096,256]{1,0:T(8,128)(2,1)} %collective-permute-done.4, pred[]{:T(512)} %eq.87), kind=kLoop, calls=%fused_computation.37 | loop fusion | flops 18874368 | bytes 8388609 | tf_op jit(solution)/shard_map/jit(_where)/select_n | solution.py:53
  68.3 368.3 %while.20 = (s32[]{:T(128)}, bf16[32,2048]{1,0:T(8,128)(2,1)S(1)}, bf16[64,2048]{1,0:T(8,128)(2,1)S(1)}, f32[2,16]{1,0:T(2,128)S(1)}, pred[]{:T(512)}, /*index=5...) while((s32[]{:T(128)}, bf16[32,2048]{1,0:T(8,128)(2,1)S(1)}, ...), condition=%wide.region_4.5_spmd.clone, body=%wide.region_0.4_spmd.clone.sunk | while | flops 1248227072 | bytes 33232504 | solution.py:113
  68.4 1.3 collective-permute-start
  69.7 5.5 %collective-permute-done = bf16[32,2048]{1,0:T(8,128)(2,1)S(1)} collective-permute-done((bf16[32,2048]{1,0:T(8,128)(2,1)S(1)}, bf16[32,2048]{1,0:T(8,128)(2,1)S(1)}, u32[]{:S(2)}, u32[]{:S(2)}) %collective-permute-start) | collective-permute-done | bytes 131104 | tf_op jit(solution)/shard_map/while/body/eval_jaxpr/ppermute | solution.py:21
  75.4 1.3 collective-permute-done.1
  76.8 1.8 collective-permute-start.2
  78.7 6.5 %collective-permute-done.2 = bf16[32,4096]{1,0:T(8,128)(2,1)S(1)} collective-permute-done((bf16[32,4096]{1,0:T(8,128)(2,1)S(1)}, bf16[32,4096]{1,0:T(8,128)(2,1)S(1)}, u32[]{:S(2)}, u32[]{:S(2)}) %collective-permute-start.2) | collective-permute-done | bytes 262176 | tf_op jit(solution)/shard_map/while/body/eval_jaxpr/ppermute | solution.py:15
  85.3 10.3 %all_to_all.38 = bf16[32,2,4096]{2,0,1:T(8,128)(2,1)S(1)} all-to-all(bf16[32,2,4096]{2,0,1:T(8,128)(2,1)S(1)} %maximum_select_fusion.14), channel_id=1, replica_groups=mesh['section'=16,'dp'=2] {'dp'}, dimensions={1} | all-to-all | bytes 1048576 | tf_op jit(solution)/shard_map/while/body/eval_jaxpr/all_to_all | solution.py:91
  95.6 11.8 %fusion.50 = f32[64,2048]{1,0:T(8,128)} fusion(bf16[64,4096]{1,0:T(8,128)(2,1)S(1)} %bitcast.44, bf16[2048,4096]{1,0:T(8,128)(2,1)} %get-tuple-element.579), kind=kOutput, calls=%fused_computation.49.clone.1 | convolution fusion | flops 1073741824 | bytes 17825792 | tf_op jit(solution)/shard_map/while/body/eval_jaxpr/dot_general | solution.py:93
  107.4 0.3 fusion.51
  107.8 2.9 convolution_multiply_fusion.2
  110.8 0.3 convolution_select_fusion.2
  111.1 30.1 %psum.15 = f32[2,16]{1,0:T(2,128)S(1)} all-reduce(f32[2,16]{1,0:T(2,128)S(1)} %convolution_select_fusion.2), channel_id=1, replica_groups=mesh['section'=16,'dp'=2] {'section'}, use_global_device_ids=true, to_apply=%region_3.3 | all-reduce | flops 32 | bytes 256 | tf_op jit(solution)/shard_map/while/body/eval_jaxpr/psum | solution.py:105
  141.2 1.0 select_dynamic-update-slice_fusion.2
  142.3 1.3 collective-permute-start
  143.6 5.5 %collective-permute-done = bf16[32,2048]{1,0:T(8,128)(2,1)S(1)} collective-permute-done((bf16[32,2048]{1,0:T(8,128)(2,1)S(1)}, bf16[32,2048]{1,0:T(8,128)(2,1)S(1)}, u32[]{:S(2)}, u32[]{:S(2)}) %collective-permute-start) | collective-permute-done | bytes 131104 | tf_op jit(solution)/shard_map/while/body/eval_jaxpr/ppermute | solution.py:21
  149.4 1.3 collective-permute-done.1
  151.0 8.3 %collective-permute-done.2 = bf16[32,4096]{1,0:T(8,128)(2,1)S(1)} collective-permute-done((bf16[32,4096]{1,0:T(8,128)(2,1)S(1)}, bf16[32,4096]{1,0:T(8,128)(2,1)S(1)}, u32[]{:S(2)}, u32[]{:S(2)}) %collective-permute-start.2) | collective-permute-done | bytes 262176 | tf_op jit(solution)/shard_map/while/body/eval_jaxpr/ppermute | solution.py:15
  159.3 10.1 %all_to_all.38 = bf16[32,2,4096]{2,0,1:T(8,128)(2,1)S(1)} all-to-all(bf16[32,2,4096]{2,0,1:T(8,128)(2,1)S(1)} %maximum_select_fusion.14), channel_id=1, replica_groups=mesh['section'=16,'dp'=2] {'dp'}, dimensions={1} | all-to-all | bytes 1048576 | tf_op jit(solution)/shard_map/while/body/eval_jaxpr/all_to_all | solution.py:91
  169.4 11.8 %fusion.50 = f32[64,2048]{1,0:T(8,128)} fusion(bf16[64,4096]{1,0:T(8,128)(2,1)S(1)} %bitcast.44, bf16[2048,4096]{1,0:T(8,128)(2,1)} %get-tuple-element.579), kind=kOutput, calls=%fused_computation.49.clone.1 | convolution fusion | flops 1073741824 | bytes 17825792 | tf_op jit(solution)/shard_map/while/body/eval_jaxpr/dot_general | solution.py:93
  181.2 0.3 fusion.51
  181.6 3.0 convolution_multiply_fusion.2
  184.7 0.3 convolution_select_fusion.2
  185.0 29.5 %psum.15 = f32[2,16]{1,0:T(2,128)S(1)} all-reduce(f32[2,16]{1,0:T(2,128)S(1)} %convolution_select_fusion.2), channel_id=1, replica_groups=mesh['section'=16,'dp'=2] {'section'}, use_global_device_ids=true, to_apply=%region_3.3 | all-reduce | flops 32 | bytes 256 | tf_op jit(solution)/shard_map/while/body/eval_jaxpr/psum | solution.py:105
  214.5 1.0 select_dynamic-update-slice_fusion.2
  215.6 1.3 collective-permute-start
  216.9 5.9 %collective-permute-done = bf16[32,2048]{1,0:T(8,128)(2,1)S(1)} collective-permute-done((bf16[32,2048]{1,0:T(8,128)(2,1)S(1)}, bf16[32,2048]{1,0:T(8,128)(2,1)S(1)}, u32[]{:S(2)}, u32[]{:S(2)}) %collective-permute-start) | collective-permute-done | bytes 131104 | tf_op jit(solution)/shard_map/while/body/eval_jaxpr/ppermute | solution.py:21
  223.1 1.3 collective-permute-done.1
  224.6 8.3 %collective-permute-done.2 = bf16[32,4096]{1,0:T(8,128)(2,1)S(1)} collective-permute-done((bf16[32,4096]{1,0:T(8,128)(2,1)S(1)}, bf16[32,4096]{1,0:T(8,128)(2,1)S(1)}, u32[]{:S(2)}, u32[]{:S(2)}) %collective-permute-start.2) | collective-permute-done | bytes 262176 | tf_op jit(solution)/shard_map/while/body/eval_jaxpr/ppermute | solution.py:15
  233.0 10.1 %all_to_all.38 = bf16[32,2,4096]{2,0,1:T(8,128)(2,1)S(1)} all-to-all(bf16[32,2,4096]{2,0,1:T(8,128)(2,1)S(1)} %maximum_select_fusion.14), channel_id=1, replica_groups=mesh['section'=16,'dp'=2] {'dp'}, dimensions={1} | all-to-all | bytes 1048576 | tf_op jit(solution)/shard_map/while/body/eval_jaxpr/all_to_all | solution.py:91
  243.1 11.8 %fusion.50 = f32[64,2048]{1,0:T(8,128)} fusion(bf16[64,4096]{1,0:T(8,128)(2,1)S(1)} %bitcast.44, bf16[2048,4096]{1,0:T(8,128)(2,1)} %get-tuple-element.579), kind=kOutput, calls=%fused_computation.49.clone.1 | convolution fusion | flops 1073741824 | bytes 17825792 | tf_op jit(solution)/shard_map/while/body/eval_jaxpr/dot_general | solution.py:93
  254.9 0.3 fusion.51
  255.3 3.0 convolution_multiply_fusion.2
  258.4 0.3 convolution_select_fusion.2
  258.7 29.5 %psum.15 = f32[2,16]{1,0:T(2,128)S(1)} all-reduce(f32[2,16]{1,0:T(2,128)S(1)} %convolution_select_fusion.2), channel_id=1, replica_groups=mesh['section'=16,'dp'=2] {'section'}, use_global_device_ids=true, to_apply=%region_3.3 | all-reduce | flops 32 | bytes 256 | tf_op jit(solution)/shard_map/while/body/eval_jaxpr/psum | solution.py:105
  288.2 1.0 select_dynamic-update-slice_fusion.2
  289.3 1.3 collective-permute-start
  290.6 5.9 %collective-permute-done = bf16[32,2048]{1,0:T(8,128)(2,1)S(1)} collective-permute-done((bf16[32,2048]{1,0:T(8,128)(2,1)S(1)}, bf16[32,2048]{1,0:T(8,128)(2,1)S(1)}, u32[]{:S(2)}, u32[]{:S(2)}) %collective-permute-start) | collective-permute-done | bytes 131104 | tf_op jit(solution)/shard_map/while/body/eval_jaxpr/ppermute | solution.py:21
  296.8 1.3 collective-permute-done.1
  298.3 8.3 %collective-permute-done.2 = bf16[32,4096]{1,0:T(8,128)(2,1)S(1)} collective-permute-done((bf16[32,4096]{1,0:T(8,128)(2,1)S(1)}, bf16[32,4096]{1,0:T(8,128)(2,1)S(1)}, u32[]{:S(2)}, u32[]{:S(2)}) %collective-permute-start.2) | collective-permute-done | bytes 262176 | tf_op jit(solution)/shard_map/while/body/eval_jaxpr/ppermute | solution.py:15
  306.7 10.1 %all_to_all.38 = bf16[32,2,4096]{2,0,1:T(8,128)(2,1)S(1)} all-to-all(bf16[32,2,4096]{2,0,1:T(8,128)(2,1)S(1)} %maximum_select_fusion.14), channel_id=1, replica_groups=mesh['section'=16,'dp'=2] {'dp'}, dimensions={1} | all-to-all | bytes 1048576 | tf_op jit(solution)/shard_map/while/body/eval_jaxpr/all_to_all | solution.py:91
  316.8 11.8 %fusion.50 = f32[64,2048]{1,0:T(8,128)} fusion(bf16[64,4096]{1,0:T(8,128)(2,1)S(1)} %bitcast.44, bf16[2048,4096]{1,0:T(8,128)(2,1)} %get-tuple-element.579), kind=kOutput, calls=%fused_computation.49.clone.1 | convolution fusion | flops 1073741824 | bytes 17825792 | tf_op jit(solution)/shard_map/while/body/eval_jaxpr/dot_general | solution.py:93
  328.6 0.3 fusion.51
  329.0 3.0 convolution_multiply_fusion.2
  332.1 0.3 convolution_select_fusion.2
  332.4 29.5 %psum.15 = f32[2,16]{1,0:T(2,128)S(1)} all-reduce(f32[2,16]{1,0:T(2,128)S(1)} %convolution_select_fusion.2), channel_id=1, replica_groups=mesh['section'=16,'dp'=2] {'section'}, use_global_device_ids=true, to_apply=%region_3.3 | all-reduce | flops 32 | bytes 256 | tf_op jit(solution)/shard_map/while/body/eval_jaxpr/psum | solution.py:105
  361.9 1.0 select_dynamic-update-slice_fusion.2
  363.0 1.3 collective-permute-start
  364.3 5.9 %collective-permute-done = bf16[32,2048]{1,0:T(8,128)(2,1)S(1)} collective-permute-done((bf16[32,2048]{1,0:T(8,128)(2,1)S(1)}, bf16[32,2048]{1,0:T(8,128)(2,1)S(1)}, u32[]{:S(2)}, u32[]{:S(2)}) %collective-permute-start) | collective-permute-done | bytes 131104 | tf_op jit(solution)/shard_map/while/body/eval_jaxpr/ppermute | solution.py:21
  370.5 1.3 collective-permute-done.1
  372.0 8.3 %collective-permute-done.2 = bf16[32,4096]{1,0:T(8,128)(2,1)S(1)} collective-permute-done((bf16[32,4096]{1,0:T(8,128)(2,1)S(1)}, bf16[32,4096]{1,0:T(8,128)(2,1)S(1)}, u32[]{:S(2)}, u32[]{:S(2)}) %collective-permute-start.2) | collective-permute-done | bytes 262176 | tf_op jit(solution)/shard_map/while/body/eval_jaxpr/ppermute | solution.py:15
  380.4 10.1 %all_to_all.38 = bf16[32,2,4096]{2,0,1:T(8,128)(2,1)S(1)} all-to-all(bf16[32,2,4096]{2,0,1:T(8,128)(2,1)S(1)} %maximum_select_fusion.14), channel_id=1, replica_groups=mesh['section'=16,'dp'=2] {'dp'}, dimensions={1} | all-to-all | bytes 1048576 | tf_op jit(solution)/shard_map/while/body/eval_jaxpr/all_to_all | solution.py:91
  390.5 11.8 %fusion.50 = f32[64,2048]{1,0:T(8,128)} fusion(bf16[64,4096]{1,0:T(8,128)(2,1)S(1)} %bitcast.44, bf16[2048,4096]{1,0:T(8,128)(2,1)} %get-tuple-element.579), kind=kOutput, calls=%fused_computation.49.clone.1 | convolution fusion | flops 1073741824 | bytes 17825792 | tf_op jit(solution)/shard_map/while/body/eval_jaxpr/dot_general | solution.py:93
  402.3 0.3 fusion.51
  402.7 3.0 convolution_multiply_fusion.2
  406.0 29.5 %psum.15 = f32[2,16]{1,0:T(2,128)S(1)} all-reduce(f32[2,16]{1,0:T(2,128)S(1)} %convolution_select_fusion.2), channel_id=1, replica_groups=mesh['section'=16,'dp'=2] {'section'}, use_global_device_ids=true, to_apply=%region_3.3 | all-reduce | flops 32 | bytes 256 | tf_op jit(solution)/shard_map/while/body/eval_jaxpr/psum | solution.py:105
  435.6 1.0 select_dynamic-update-slice_fusion.2
  436.6 0.7 copy-done.1
  (93 shorter events, 4.4 us)
Async XLA Ops:
  7.2 9.3 %copy-start.5 = (s32[2]{0:T(128)S(1)}, s32[2]{0:T(128)}, u32[]{:S(2)}) copy-start(s32[2]{0:T(128)} %param.11) | copy-start | bytes 28
  7.2 9.3 %copy-start.6 = (s32[64]{0:T(128)S(1)}, s32[64]{0:T(128)}, u32[]{:S(2)}) copy-start(s32[64]{0:T(128)} %param.12) | copy-start | bytes 772
  7.2 3.1 collective-permute-start.3
  13.6 49.1 %collective-permute-start.4 = (bf16[4096,256]{1,0:T(8,128)(2,1)}, bf16[4096,256]{1,0:T(8,128)(2,1)}, u32[]{:S(2)}, u32[]{:S(2)}) collective-permute-start(bf16[4096,256]{1,0:T(8,128)(2,1)} %maximum_select_fusion.6), channel_id=1, source_target_pairs={{0,4},{2,6},{4,0},{6,2},{8,12},{10,14},{12,8},{14,10},{16,20},{18,... | collective-permute-start | bytes 6291464 | tf_op jit(solution)/shard_map/ppermute | solution.py:15
  17.8 50.5 %copy-start = (bf16[2048,256]{1,0:T(8,128)(2,1)S(1)}, bf16[2048,256]{1,0:T(8,128)(2,1)}, u32[]{:S(2)}) copy-start(bf16[2048,256]{1,0:T(8,128)(2,1)} %param.16) | copy-start | bytes 3145732
  17.8 50.5 %copy-start.2 = (bf16[64,2048]{1,0:T(8,128)(2,1)S(1)}, bf16[64,2048]{1,0:T(8,128)(2,1)}, u32[]{:S(2)}) copy-start(bf16[64,2048]{1,0:T(8,128)(2,1)} %param.13) | copy-start | bytes 786436
  17.8 50.5 %copy-start.3 = (bf16[64,2048]{1,0:T(8,128)(2,1)S(1)}, bf16[64,2048]{1,0:T(8,128)(2,1)}, u32[]{:S(2)}) copy-start(bf16[64,2048]{1,0:T(8,128)(2,1)} %param.14) | copy-start | bytes 786436
  68.3 72.9 %reduce-scatter.2.cloned.1.call-start = ((), (), s32[]{:S(2)}) async-start(), calls=%async_computation.2 | async-start | bytes 786432 | tf_op jit(solution)/shard_map/while/body/eval_jaxpr/reduce_scatter | solution.py:92
  68.4 6.9 %collective-permute-start = (bf16[32,2048]{1,0:T(8,128)(2,1)S(1)}, bf16[32,2048]{1,0:T(8,128)(2,1)S(1)}, u32[]{:S(2)}, u32[]{:S(2)}) collective-permute-start(bf16[32,2048]{1,0:T(8,128)(2,1)S(1)} %broadcast_select_fusion.2), channel_id=1, source_target_pairs={{8,0},{10,2},{12,4},{14,6},{16,8},{18,10},{20,12},{22,14},{24,16},... | collective-permute-start | bytes 393224 | tf_op jit(solution)/shard_map/while/body/eval_jaxpr/ppermute | solution.py:21
  75.3 1.4 collective-permute-start.1
  76.8 8.4 %collective-permute-start.2 = (bf16[32,4096]{1,0:T(8,128)(2,1)S(1)}, bf16[32,4096]{1,0:T(8,128)(2,1)S(1)}, u32[]{:S(2)}, u32[]{:S(2)}) collective-permute-start(bf16[32,4096]{1,0:T(8,128)(2,1)S(1)} %maximum_select_fusion.13), channel_id=1, source_target_pairs={{0,4},{2,6},{4,0},{6,2},{8,12},{10,14},{12,8},{14,10},{16,20},{18,... | collective-permute-start | bytes 786440 | tf_op jit(solution)/shard_map/while/body/eval_jaxpr/ppermute | solution.py:15
  142.2 72.2 %reduce-scatter.2.cloned.1.call-start = ((), (), s32[]{:S(2)}) async-start(), calls=%async_computation.2 | async-start | bytes 786432 | tf_op jit(solution)/shard_map/while/body/eval_jaxpr/reduce_scatter | solution.py:92
  142.3 6.9 %collective-permute-start = (bf16[32,2048]{1,0:T(8,128)(2,1)S(1)}, bf16[32,2048]{1,0:T(8,128)(2,1)S(1)}, u32[]{:S(2)}, u32[]{:S(2)}) collective-permute-start(bf16[32,2048]{1,0:T(8,128)(2,1)S(1)} %broadcast_select_fusion.2), channel_id=1, source_target_pairs={{8,0},{10,2},{12,4},{14,6},{16,8},{18,10},{20,12},{22,14},{24,16},... | collective-permute-start | bytes 393224 | tf_op jit(solution)/shard_map/while/body/eval_jaxpr/ppermute | solution.py:21
  149.3 1.4 collective-permute-start.1
  150.8 8.4 %collective-permute-start.2 = (bf16[32,4096]{1,0:T(8,128)(2,1)S(1)}, bf16[32,4096]{1,0:T(8,128)(2,1)S(1)}, u32[]{:S(2)}, u32[]{:S(2)}) collective-permute-start(bf16[32,4096]{1,0:T(8,128)(2,1)S(1)} %maximum_select_fusion.13), channel_id=1, source_target_pairs={{0,4},{2,6},{4,0},{6,2},{8,12},{10,14},{12,8},{14,10},{16,20},{18,... | collective-permute-start | bytes 786440 | tf_op jit(solution)/shard_map/while/body/eval_jaxpr/ppermute | solution.py:15
  215.5 72.6 %reduce-scatter.2.cloned.1.call-start = ((), (), s32[]{:S(2)}) async-start(), calls=%async_computation.2 | async-start | bytes 786432 | tf_op jit(solution)/shard_map/while/body/eval_jaxpr/reduce_scatter | solution.py:92
  215.6 7.3 %collective-permute-start = (bf16[32,2048]{1,0:T(8,128)(2,1)S(1)}, bf16[32,2048]{1,0:T(8,128)(2,1)S(1)}, u32[]{:S(2)}, u32[]{:S(2)}) collective-permute-start(bf16[32,2048]{1,0:T(8,128)(2,1)S(1)} %broadcast_select_fusion.2), channel_id=1, source_target_pairs={{8,0},{10,2},{12,4},{14,6},{16,8},{18,10},{20,12},{22,14},{24,16},... | collective-permute-start | bytes 393224 | tf_op jit(solution)/shard_map/while/body/eval_jaxpr/ppermute | solution.py:21
  223.0 1.4 collective-permute-start.1
  224.5 8.4 %collective-permute-start.2 = (bf16[32,4096]{1,0:T(8,128)(2,1)S(1)}, bf16[32,4096]{1,0:T(8,128)(2,1)S(1)}, u32[]{:S(2)}, u32[]{:S(2)}) collective-permute-start(bf16[32,4096]{1,0:T(8,128)(2,1)S(1)} %maximum_select_fusion.13), channel_id=1, source_target_pairs={{0,4},{2,6},{4,0},{6,2},{8,12},{10,14},{12,8},{14,10},{16,20},{18,... | collective-permute-start | bytes 786440 | tf_op jit(solution)/shard_map/while/body/eval_jaxpr/ppermute | solution.py:15
  289.2 72.6 %reduce-scatter.2.cloned.1.call-start = ((), (), s32[]{:S(2)}) async-start(), calls=%async_computation.2 | async-start | bytes 786432 | tf_op jit(solution)/shard_map/while/body/eval_jaxpr/reduce_scatter | solution.py:92
  289.3 7.3 %collective-permute-start = (bf16[32,2048]{1,0:T(8,128)(2,1)S(1)}, bf16[32,2048]{1,0:T(8,128)(2,1)S(1)}, u32[]{:S(2)}, u32[]{:S(2)}) collective-permute-start(bf16[32,2048]{1,0:T(8,128)(2,1)S(1)} %broadcast_select_fusion.2), channel_id=1, source_target_pairs={{8,0},{10,2},{12,4},{14,6},{16,8},{18,10},{20,12},{22,14},{24,16},... | collective-permute-start | bytes 393224 | tf_op jit(solution)/shard_map/while/body/eval_jaxpr/ppermute | solution.py:21
  296.7 1.4 collective-permute-start.1
  298.2 8.4 %collective-permute-start.2 = (bf16[32,4096]{1,0:T(8,128)(2,1)S(1)}, bf16[32,4096]{1,0:T(8,128)(2,1)S(1)}, u32[]{:S(2)}, u32[]{:S(2)}) collective-permute-start(bf16[32,4096]{1,0:T(8,128)(2,1)S(1)} %maximum_select_fusion.13), channel_id=1, source_target_pairs={{0,4},{2,6},{4,0},{6,2},{8,12},{10,14},{12,8},{14,10},{16,20},{18,... | collective-permute-start | bytes 786440 | tf_op jit(solution)/shard_map/while/body/eval_jaxpr/ppermute | solution.py:15
  362.9 72.6 %reduce-scatter.2.cloned.1.call-start = ((), (), s32[]{:S(2)}) async-start(), calls=%async_computation.2 | async-start | bytes 786432 | tf_op jit(solution)/shard_map/while/body/eval_jaxpr/reduce_scatter | solution.py:92
  363.0 7.3 %collective-permute-start = (bf16[32,2048]{1,0:T(8,128)(2,1)S(1)}, bf16[32,2048]{1,0:T(8,128)(2,1)S(1)}, u32[]{:S(2)}, u32[]{:S(2)}) collective-permute-start(bf16[32,2048]{1,0:T(8,128)(2,1)S(1)} %broadcast_select_fusion.2), channel_id=1, source_target_pairs={{8,0},{10,2},{12,4},{14,6},{16,8},{18,10},{20,12},{22,14},{24,16},... | collective-permute-start | bytes 393224 | tf_op jit(solution)/shard_map/while/body/eval_jaxpr/ppermute | solution.py:21
  370.4 1.4 collective-permute-start.1
  371.9 8.4 %collective-permute-start.2 = (bf16[32,4096]{1,0:T(8,128)(2,1)S(1)}, bf16[32,4096]{1,0:T(8,128)(2,1)S(1)}, u32[]{:S(2)}, u32[]{:S(2)}) collective-permute-start(bf16[32,4096]{1,0:T(8,128)(2,1)S(1)} %maximum_select_fusion.13), channel_id=1, source_target_pairs={{0,4},{2,6},{4,0},{6,2},{8,12},{10,14},{12,8},{14,10},{16,20},{18,... | collective-permute-start | bytes 786440 | tf_op jit(solution)/shard_map/while/body/eval_jaxpr/ppermute | solution.py:15
  436.6 0.7 copy-start.1
  436.6 0.7 copy-start.4
Sparse Core Ops, SparseCore 0:
  107.5 14.0 reduce-scatter.1
  181.4 10.9 reduce-scatter.1
  255.0 10.9 reduce-scatter.1
  328.7 10.9 reduce-scatter.1
  402.4 10.9 reduce-scatter.1
where the time goes:
time: 445 us; the launch traced here: 444 us
  blocking collectives  199 us (45%)
  waiting for transfers between devices  123 us (28%)
  matrix products  76.6 us (17%)
  other arithmetic  17.1 us (4%)
  between operations  13.8 us (3%)
  starting transfers between devices  12.5 us (3%)
    psum x5, blocking collectives, advance(): totals = totals + lax.psum(increment, 'section')  148 us
    ppermute x12, waiting for transfers between devices, from_partner(): return lax.ppermute(value, axis, pairs)  93.7 us
    dot_general x5, matrix products, advance(): lax.dot_general(by_group, weights, (((1,), (1,)), ((), ())), preferred_el...  58.9 us
    all_to_all x5, blocking collectives, advance(): lax.all_to_all(gate_full, 'dp', split_axis=1, concat_axis=0, tiled=True)  50.8 us
    ppermute x5, waiting for transfers between devices, from_behind(): lax.ppermute(value, axis, [(source, source + steps) for source in range(f...  28.9 us
    dot_general x5, matrix products, score_terms(): jnp.dot(gate_full, right_full, preferred_element_type=jnp.float32)  14.9 us
  transfers between devices with their start and end apart: 22, of which 17 were waited for; matrix products, arithmetic and copies ran while one was open for 5% of the time, Pallas kernels for 0%

commit v1 on v0

v1 whole, which is shorter than its diff:
```python
import jax
import jax.numpy as jnp
from jax import lax
from jax.experimental import pallas as pl
from jax.experimental.pallas import tpu as pltpu
from jax.sharding import PartitionSpec as P

LAYERS = 4
QUERIES = 16
RANK = 16
CHUNKS = 2
AXES = ("section", "dp")


def spot():
    groups = lax.axis_size("dp")
    blocks = lax.axis_size("section") // LAYERS
    cores = blocks // groups
    position = lax.axis_index("section")
    block = lax.rem(position, blocks)
    return (
        lax.div(position, blocks),
        block,
        lax.div(block, cores),
        lax.rem(block, cores),
        lax.axis_index("dp"),
    )


def silu_slope(preact):
    sigmoid_value = jax.nn.sigmoid(preact)
    return sigmoid_value * (1.0 + preact * (1.0 - sigmoid_value))


VMEM = pl.BlockSpec(memory_space=pltpu.VMEM)
HBM = pl.BlockSpec(memory_space=pltpu.HBM)
ANY = pl.BlockSpec(memory_space=pl.ANY)


def small():
    return pltpu.CompilerParams(vmem_limit_bytes=12 * 2**20)


def load(weights, chunk, cores, after=(), pieces=8):
    rows = weights.shape[0] // pieces
    part = weights.shape[1] // (cores * CHUNKS)

    def body(weight_ref, *refs):
        out_ref, sems = refs[-2:]
        copies = []
        for k in range(cores):
            for i in range(pieces):
                span = pl.ds(i * rows, rows)
                source = weight_ref.at[span, pl.ds((k * CHUNKS + chunk) * part, part)]
                goal = out_ref.at[span, pl.ds(k * part, part)]
                copies.append(pltpu.make_async_copy(source, goal, sems.at[k, i]))
        for copy in copies:
            copy.start()
        for copy in copies:
            copy.wait()

    return pl.pallas_call(
        body,
        in_specs=[HBM] + [ANY] * len(after),
        out_specs=VMEM,
        out_shape=pltpu.VMEM((weights.shape[0], cores * part), weights.dtype),
        scratch_shapes=[pltpu.SemaphoreType.DMA((cores, pieces))],
        compiler_params=small(),
    )(pltpu.with_memory_space_constraint(weights, pltpu.HBM), *after)


def begin(lengths, ids, preacts, cotangent):
    tokens, width = preacts.shape
    part = width // CHUNKS
    seqs = lengths.shape[0]

    def body(length_ref, id_ref, preact_ref, cotangent_ref, *refs):
        layer, block, _, _, group = spot()
        top_ref = refs[0]
        buffer, sem, preact_buffer, preact_sem = refs[-8:-4]
        id_buffer, id_sem, length_buffer, length_sem = refs[-4:]
        column = pl.multiple_of(block * width, width)
        copy = pltpu.make_async_copy(cotangent_ref.at[:, pl.ds(column, width)], buffer, sem)
        copies = [
            copy,
            pltpu.make_async_copy(preact_ref, preact_buffer, preact_sem),
            pltpu.make_async_copy(id_ref, id_buffer, id_sem),
            pltpu.make_async_copy(length_ref, length_buffer, length_sem),
        ]
        for one in copies:
            one.start()
        for one in copies:
            one.wait()
        preact = preact_buffer[...]
        slope = silu_slope(preact.astype(jnp.float32))
        scale = jnp.zeros((1, tokens), jnp.float32)
        for n in range(seqs):
            count = jnp.full((1, tokens), length_buffer[n], jnp.int32).astype(jnp.float32)
            mine = id_buffer[...] == group * seqs + n
            scale = jnp.where(mine, 1.0 / jnp.maximum(count, 1.0), scale)
        row = lax.broadcasted_iota(jnp.int32, (tokens, tokens), 0)
        lane = lax.broadcasted_iota(jnp.int32, (tokens, tokens), 1)
        scale = jnp.sum(jnp.where(row == lane, scale, 0.0), axis=1, keepdims=True)
        top = (buffer[...].astype(jnp.float32) * scale).astype(jnp.bfloat16)
        top_ref[...] = top
        gate = (slope * top.astype(jnp.float32)).astype(jnp.bfloat16)
        value = jnp.where(layer == LAYERS - 1, gate, preact)
        for n in range(CHUNKS):
            refs[1 + n][...] = value[:, n * part : (n + 1) * part]

    outs = pl.pallas_call(
        body,
        in_specs=[HBM, HBM, HBM, HBM],
        out_specs=[VMEM] * (1 + CHUNKS),
        out_shape=[jax.ShapeDtypeStruct((tokens, width), jnp.bfloat16)]
        + [jax.ShapeDtypeStruct((tokens, part), jnp.bfloat16)] * CHUNKS,
        scratch_shapes=[
            pltpu.VMEM((tokens, width), jnp.bfloat16),
            pltpu.SemaphoreType.DMA(()),
            pltpu.VMEM((tokens, width), jnp.bfloat16),
            pltpu.SemaphoreType.DMA(()),
            pltpu.VMEM((1, tokens), jnp.int32),
            pltpu.SemaphoreType.DMA(()),
            pltpu.SMEM((seqs,), jnp.int32),
            pltpu.SemaphoreType.DMA(()),
        ],
        compiler_params=small(),
    )(
        *[
            pltpu.with_memory_space_constraint(value, pltpu.HBM)
            for value in (lengths, ids, preacts, cotangent)
        ],
    )
    return outs[0], outs[1:]


def product_body(
    lhs_ref, weight_ref, *refs, tick, distance, first_row, row_count, groups, cores, has_acc, splits
):
    outs = refs[1:] if has_acc else refs
    width = lhs_ref.shape[1]
    layer, _, place, core, group = spot()
    column = pl.multiple_of(lax.rem(core + distance, cores) * width, width)
    tile = min(512, row_count)

    @pl.when(layer == LAYERS - 1 - tick)
    def _():
        lhs = lhs_ref[...]
        for start in range(0, row_count, tile):
            weight = weight_ref[pl.ds(first_row + start, tile), pl.ds(column, width)]
            value = lax.dot_general(
                weight, lhs, (((1,), (1,)), ((), ())), preferred_element_type=jnp.float32
            )
            if has_acc:
                value = value + refs[0][pl.ds(first_row + start, tile), :]
            if splits:
                outs[-1][:, pl.ds(start, tile)] = value.T
            else:
                outs[0][pl.ds(start, tile), :] = value
        if splits:
            count = lhs.shape[0] // groups
            for slot in range(groups):
                first = pl.multiple_of(lax.rem(group + slot - place + groups, groups) * count, count)
                outs[slot][...] = outs[-1][pl.ds(first, count), :].astype(outs[slot].dtype)


def product(
    lhs, weights, acc, tick, distance, first_row, row_count, groups, cores, splits, after=()
):
    tokens = lhs.shape[0]
    width = lhs.shape[1]
    specs = [VMEM, VMEM]
    operands = [lhs, pltpu.with_memory_space_constraint(weights, pltpu.VMEM)]
    if acc is not None:
        specs.append(VMEM)
        operands.append(pltpu.with_memory_space_constraint(acc, pltpu.VMEM))
    used = len(specs)
    specs += [ANY] * len(after)
    operands += after
    scratch = []
    if splits:
        rows = tokens // groups
        kinds = [jnp.float32] + [jnp.bfloat16] * (groups - 1)
        out_shape = [jax.ShapeDtypeStruct((rows, row_count), kind) for kind in kinds]
        out_specs = [VMEM for _ in kinds]
        scratch = [pltpu.VMEM((tokens, row_count), jnp.float32)]
    else:
        out_shape = pltpu.VMEM((row_count, tokens), jnp.float32)
        out_specs = VMEM

    def body(*refs):
        product_body(
            *refs[:used],
            *refs[used + len(after) :],
            tick=tick,
            distance=distance,
            first_row=first_row,
            row_count=row_count,
            groups=groups,
            cores=cores,
            has_acc=acc is not None,
            splits=splits,
        )

    return pl.pallas_call(
        body,
        in_specs=specs,
        out_specs=out_specs,
        scratch_shapes=scratch,
        out_shape=out_shape,
        compiler_params=small(),
        cost_estimate=pl.CostEstimate(
            flops=2 * tokens * width * row_count,
            bytes_accessed=2 * width * row_count,
            transcendentals=0,
        ),
    )(*operands)


def join(pieces, after):
    rows, width = pieces[0].shape

    def body(*refs):
        for n in range(len(pieces)):
            refs[-1][pl.ds(n * rows, rows), :] = refs[n][...]

    return pl.pallas_call(
        body,
        in_specs=[VMEM] * len(pieces) + [ANY] * len(after),
        out_specs=VMEM,
        out_shape=jax.ShapeDtypeStruct((rows * len(pieces), width), pieces[0].dtype),
        compiler_params=small(),
    )(*pieces, *after)


def combine(kept, arrived, residual, column, before):
    rows, width = kept.shape
    parts = len(arrived)

    def body(*refs):
        total = refs[0][...] + refs[1 + parts][:, pl.ds(column, width)].astype(jnp.float32)
        for ref in refs[1 : 1 + parts]:
            total = total + ref[...].astype(jnp.float32)
        value = total.astype(jnp.bfloat16)
        if before:
            outs = refs[2 + parts + len(before) :]
            for n in range(len(before)):
                outs[1][:, pl.ds(n * width, width)] = refs[2 + parts + n][...]
            outs[1][:, pl.ds(column, width)] = value
        else:
            outs = refs[2 + parts :]
        outs[0][...] = value

    out_shape = [jax.ShapeDtypeStruct((rows, width), jnp.bfloat16)]
    if before:
        out_shape.append(jax.ShapeDtypeStruct(residual.shape, jnp.bfloat16))
    operands = [kept, *arrived, residual, *before]
    return pl.pallas_call(
        body,
        in_specs=[VMEM] * len(operands),
        out_specs=[VMEM] * len(out_shape),
        out_shape=out_shape,
        compiler_params=small(),
    )(*operands)


def finish(parts, arrived, residual, earlier):
    rows = residual.shape[0]
    width = parts[0].shape[1]
    count = len(parts)
    per_part = len(arrived[0])

    def body(*refs):
        layer = spot()[0]
        out_ref = refs[-1]
        residual_ref = refs[count * (1 + per_part)]
        earlier_refs = refs[count * (1 + per_part) + 1 : -1]
        for n in range(count):
            span = pl.ds(n * width, width)
            total = refs[n][...] + residual_ref[:, span].astype(jnp.float32)
            for d in range(per_part):
                total = total + refs[count + n * per_part + d][...].astype(jnp.float32)
            value = total.astype(jnp.bfloat16)
            for tick, ref in enumerate(earlier_refs):
                value = jnp.where(layer == LAYERS - 1 - tick, ref[:, span], value)
            out_ref[:, span] = value

    operands = [*parts]
    for group in arrived:
        operands += group
    operands += [residual, *earlier]
    return pl.pallas_call(
        body,
        in_specs=[VMEM] * len(operands),
        out_specs=VMEM,
        out_shape=jax.ShapeDtypeStruct((rows, width * count), jnp.bfloat16),
        compiler_params=small(),
    )(*operands)


def left_side(values, factors):
    def body(value_ref, factor_ref, out_ref):
        out_ref[...] = jnp.dot(
            value_ref[...], factor_ref[...], preferred_element_type=jnp.float32
        )

    return pl.pallas_call(
        body,
        in_specs=[VMEM, VMEM],
        out_specs=VMEM,
        out_shape=jax.ShapeDtypeStruct((values.shape[0], factors.shape[1]), jnp.float32),
        compiler_params=small(),
    )(values, factors)


def score_terms(ids, preacts, candidates, factors, left, seqs):
    def body(id_ref, preact_ref, *refs):
        layer, _, _, _, group = spot()
        factor_ref, left_ref, out_ref = refs[-3:]
        value = refs[0][...]
        for tick, ref in enumerate(refs[1:-3]):
            value = jnp.where(layer == LAYERS - 2 - tick, ref[...], value)
        slope = silu_slope(preact_ref[...].astype(jnp.float32))
        gate = (slope * value.astype(jnp.float32)).astype(jnp.bfloat16)
        right = jnp.dot(gate, factor_ref[...], preferred_element_type=jnp.float32)
        terms = left_ref[...] * right
        rank = lax.broadcasted_iota(jnp.int32, (terms.shape[1], QUERIES), 0) // RANK
        query = lax.broadcasted_iota(jnp.int32, (terms.shape[1], QUERIES), 1)
        pick = (rank == query).astype(jnp.float32)
        tokens = terms.shape[0]
        slot = group * seqs + lax.broadcasted_iota(jnp.int32, (seqs, tokens), 0)
        member = (id_ref[...] == slot).astype(jnp.float32)
        total = jnp.dot(
            member, terms, preferred_element_type=jnp.float32, precision=lax.Precision.HIGHEST
        )
        out_ref[...] = jnp.dot(
            total, pick, preferred_element_type=jnp.float32, precision=lax.Precision.HIGHEST
        )

    operands = [ids, preacts, *candidates, factors, left]
    return pl.pallas_call(
        body,
        in_specs=[VMEM] * len(operands),
        out_specs=VMEM,
        out_shape=jax.ShapeDtypeStruct((seqs, QUERIES), jnp.float32),
        compiler_params=small(),
    )(*operands)


def per_device(
    cotangent, lengths, example_ids, layer_inputs, preacts, weights, query_left, query_right
):
    blocks = lax.axis_size("section") // LAYERS
    groups = lax.axis_size("dp")
    cores = blocks // groups
    tokens = cotangent.shape[0]
    width = layer_inputs.shape[1]
    part = width // CHUNKS
    seqs = lengths.shape[0]

    def device(s, h, k, y):
        return ((s * blocks) + h * cores + k) * groups + y

    everyone = [
        (s, h, k, y)
        for s in range(LAYERS)
        for h in range(groups)
        for k in range(cores)
        for y in range(groups)
    ]

    def send(value, target):
        pairs = []
        for spot in everyone:
            goal = target(*spot)
            if goal[0] >= 0:
                pairs.append((device(*spot), device(*goal)))
        return lax.ppermute(value, AXES, pairs)

    def turned(value):
        return send(value, lambda s, h, k, y: (s, y, k, h))

    def lowered(value, tick, turn):
        def target(s, h, k, y):
            if s != LAYERS - 1 - tick:
                return (-1, 0, 0, 0)
            return (s - 1, y, k, h) if turn else (s - 1, h, k, y)

        return send(value, target)

    def from_places(value):
        return [
            send(value, lambda s, h, k, y: (s, (h - d) % groups, k, y))
            for d in range(1, groups)
        ]

    def from_cores(value):
        return [
            send(value, lambda s, h, k, y: (s, h, (k - d) % cores, y)) for d in range(1, cores)
        ]

    def sum_over(value, axis, count):
        step = 1
        while step < count:
            if axis == "core":
                value = value + send(value, lambda s, h, k, y: (s, h, k ^ step, y))
            elif axis == "place":
                value = value + send(value, lambda s, h, k, y: (s, h ^ step, k, y))
            else:
                value = value + send(value, lambda s, h, k, y: (s ^ step, h, k, y))
            step *= 2
        return value

    id_row = example_ids.reshape(1, tokens)
    top_grad, payload = begin(lengths, id_row, preacts, cotangent)

    turned_payload = [turned(payload[o]) for o in range(CHUNKS)]
    slope_turned = [silu_slope(value.astype(jnp.float32)) for value in turned_payload]
    held = [load(weights, 0, cores, [turned_payload[0]])]
    gates = [turned_payload[0]]
    for o in range(1, CHUNKS):
        gates.append(join([turned_payload[o]], [held[o - 1]]))
        held.append(load(weights, o, cores, [gates[o]]))
    left_sum = left_side(layer_inputs, query_left)
    residual = top_grad
    candidates = [top_grad]
    sums = []
    for tick in range(LAYERS):
        last = tick == LAYERS - 1
        acc = None
        parts = []
        mine_sent = [from_places(gates[o]) for o in range(CHUNKS)]
        behind = []
        if tick == 1:
            left_sum = sum_over(left_sum, "core", cores)
            behind = [left_sum]
        if tick == 2:
            left_sum = sum_over(left_sum, "place", groups)
            behind = [left_sum]
        if last:
            terms = score_terms(id_row, preacts, candidates, query_right, left_sum, seqs)
            terms = sum_over(terms, "core", cores)
            behind = [terms]
            terms = sum_over(terms, "place", groups)
        for o in range(CHUNKS):
            mine = join([gates[o]] + mine_sent[o], [] if acc is None else [acc])
            pieces = [mine] + from_cores(mine)
            for k in range(cores):
                if o == CHUNKS - 1 and k == cores - 1:
                    for n in range(CHUNKS):
                        parts.append(
                            product(
                                pieces[k], held[o], acc, tick, k, n * part, part, groups, cores,
                                True, behind + [p[0] for p in parts[:n]],
                            )
                        )
                else:
                    acc = product(
                        pieces[k], held[o], acc, tick, k, 0, width, groups, cores, False,
                        held[1:] if tick + o + k == 0 else [],
                    )
        arrived = []
        for n in range(CHUNKS):
            arrived.append(
                [
                    send(parts[n][d], lambda s, h, k, y: (s, h, k, (y + d) % groups))
                    for d in range(1, groups)
                ]
            )
        kept = [piece[0] for piece in parts]
        if last:
            break
        in_parts = []
        for n in range(CHUNKS):
            outs = combine(
                kept[n], arrived[n], residual, n * part, in_parts if n == CHUNKS - 1 else []
            )
            in_parts.append(outs[0])
        in_grad = outs[1]
        sums.append(in_grad)
        gates = []
        for n in range(CHUNKS):
            came = lowered(in_parts[n], tick, True)
            gates.append((slope_turned[n] * came.astype(jnp.float32)).astype(jnp.bfloat16))
        residual = lowered(in_grad, tick, False)
        candidates.append(residual)

    result = finish(kept, arrived, residual, sums)
    scores = sum_over(terms, "layer", LAYERS)
    return (result, scores)


def solution(mesh):
    placed = (
        P("dp", None),
        P("dp"),
        P("dp"),
        P("dp", "section"),
        P("dp", "section"),
        P("section", "dp"),
        P("section", None),
        P("section", None),
    )
    return jax.shard_map(
        per_device,
        mesh=mesh,
        in_specs=placed,
        out_specs=(P("dp", "section"), P("dp", None)),
        check_vma=False,
    )
```

time: 445 us -> 152 us (0.34)
  blocking collectives: 199 us -> 0 us
  matrix products: 76.6 us -> 0 us
  waiting for transfers between devices: 123 us -> 85.5 us
  starting transfers between devices: 12.5 us -> 46.8 us
  Pallas kernels: 0 us -> 16.6 us
  other arithmetic: 17.1 us -> 1.28 us
  between operations: 13.8 us -> 1.17 us
    psum x5 -> x0, blocking collectives: 148 us -> none  [advance(): totals = totals + lax.psum(increment, 'section')]
    dot_general x21 -> x0, matrix products: 76.6 us -> none  [the longest x5 58.9 us: advance(): lax.dot_general(by_group, weights, (((1,), (1,)), ((), ())), preferred_el...]
    all_to_all x5 -> x0, blocking collectives: 50.8 us -> none  [advance(): lax.all_to_all(gate_full, 'dp', split_axis=1, concat_axis=0, tiled=True)]
    ppermute x17 -> x41, waiting for transfers between devices: 123 us -> 85.5 us  [send(): return lax.ppermute(value, AXES, pairs)]
    ppermute x17 -> x41, starting transfers between devices: 12.3 us -> 46.8 us  [send(): return lax.ppermute(value, AXES, pairs)]
    pallas_call x0 -> x41, Pallas kernels: none -> 16.6 us  [the longest x2 7.09 us: load(): pl.pallas_call(body, in_specs=[HBM] + [ANY] * len(after), out_specs=VMEM,...]
    select_n x22 -> x0, other arithmetic: 15.1 us -> none  [the longest x2 8.88 us: per_device(): jnp.where(upper_half == 1, jnp.concatenate([partner, right_full], 0), jnp...]
  transfers between devices with their start and end apart: 22 -> 41, of which waited for: 17 -> 22; matrix products, arithmetic and copies ran while one was open for 5% -> 1% of each run, Pallas kernels for 0% -> 8%
where the time goes in v1:
time: 152 us; the launch traced here: 151 us
  waiting for transfers between devices  85.5 us (56%)
  starting transfers between devices  46.8 us (31%)
  Pallas kernels  16.6 us (11%)
    ppermute x41, waiting for transfers between devices, send(): return lax.ppermute(value, AXES, pairs)  85.5 us
    ppermute x41, starting transfers between devices, send(): return lax.ppermute(value, AXES, pairs)  46.8 us
    pallas_call x2, Pallas kernels, load(): pl.pallas_call(body, in_specs=[HBM] + [ANY] * len(after), out_specs=VMEM,...  7.09 us
    pallas_call x20, Pallas kernels, product(): pl.pallas_call(body, in_specs=specs, out_specs=out_specs, scratch_shapes=...  5.76 us
  transfers between devices with their start and end apart: 41, of which 22 were waited for; matrix products, arithmetic and copies ran while one was open for 1% of the time, Pallas kernels for 8%

profile of v1, /device:TPU:0, one launch (start us, length us, event | category | flops | bytes accessed | tf_op | source)
XLA Modules:
  0.0 151.4 jit_solution(2099886839185043098)
XLA Ops:
  0.6 1.5 shard_map.95
  2.1 0.7 collective-permute-start.1
  2.8 10.3 %collective-permute-start.3 = (bf16[64,1024]{1,0:T(8,128)(2,1)S(1)}, bf16[64,1024]{1,0:T(8,128)(2,1)S(1)}, u32[]{:S(2)}, u32[]{:S(2)}) collective-permute-start(bf16[64,1024]{1,0:T(8,128)(2,1)S(1)} %collective-permute-done.1.refs_0_), channel_id=1, source_target_pairs={{0,4},{1,5},{2,6},{3,7},{4,0},{5,1},{6,2},{7,3},{8,12},{9,13},{10,... | collective-permute-start | bytes 393224 | tf_op jit(solution)/shard_map/ppermute | solution.py:378
  13.1 2.9 %collective-permute-done.3.refs_1_ = bf16[64,1024]{1,0:T(8,128)(2,1)S(1)} collective-permute-done((bf16[64,1024]{1,0:T(8,128)(2,1)S(1)}, bf16[64,1024]{1,0:T(8,128)(2,1)S(1)}, u32[]{:S(2)}, u32[]{:S(2)}) %collective-permute-start.3) | collective-permute-done | bytes 131104 | tf_op jit(solution)/shard_map/ppermute | solution.py:378
  16.1 0.7 collective-permute-start
  16.8 3.5 %shard_map.96.refs_1_ = bf16[2048,2048]{1,0:T(8,128)(2,1)S(1)} custom-call(bf16[2048,4096]{1,0:T(8,128)(2,1)} %weight_ref.3, bf16[64,1024]{1,0:T(8,128)(2,1)S(1)} %collective-permute-done.1.refs_0_), custom_call_target="tpu_custom_call" | custom-call | tf_op jit(solution)/shard_map/pallas_call | solution.py:62
  20.4 6.5 %collective-permute-start.2 = (bf16[64,1024]{1,0:T(8,128)(2,1)S(1)}, bf16[64,1024]{1,0:T(8,128)(2,1)S(1)}, u32[]{:S(2)}, u32[]{:S(2)}) collective-permute-start(bf16[64,1024]{1,0:T(8,128)(2,1)S(1)} %shard_map.97.refs_0_), channel_id=1, source_target_pairs={{0,4},{1,5},{2,6},{3,7},{4,0},{5,1},{6,2},{7,3},{8,12},{9,13},{10,... | collective-permute-start | bytes 393224 | tf_op jit(solution)/shard_map/ppermute | solution.py:378
  26.9 3.5 %shard_map.99.refs_2_.refs_1_ = bf16[2048,2048]{1,0:T(8,128)(2,1)S(1)} custom-call(bf16[2048,4096]{1,0:T(8,128)(2,1)} %weight_ref.3, bf16[64,1024]{1,0:T(8,128)(2,1)S(1)} %shard_map.97.refs_0_), custom_call_target="tpu_custom_call" | custom-call | tf_op jit(solution)/shard_map/pallas_call | solution.py:62
  30.7 1.5 collective-permute-done.5.refs_0_
  32.2 1.4 collective-permute-start.7
  33.6 4.1 %collective-permute-done.7.refs_1_ = bf16[64,1024]{1,0:T(8,128)(2,1)S(1)} collective-permute-done((bf16[64,1024]{1,0:T(8,128)(2,1)S(1)}, bf16[64,1024]{1,0:T(8,128)(2,1)S(1)}, u32[]{:S(2)}, u32[]{:S(2)}) %collective-permute-start.7) | collective-permute-done | bytes 131104 | tf_op jit(solution)/shard_map/ppermute | solution.py:378
  37.8 0.7 collective-permute-start.10
  38.5 1.5 collective-permute-start.6
  40.1 0.7 collective-permute-start.11
  40.8 2.7 %collective-permute-done.6.refs_1_ = bf16[64,1024]{1,0:T(8,128)(2,1)S(1)} collective-permute-done((bf16[64,1024]{1,0:T(8,128)(2,1)S(1)}, bf16[64,1024]{1,0:T(8,128)(2,1)S(1)}, u32[]{:S(2)}, u32[]{:S(2)}) %collective-permute-start.6) | collective-permute-done | bytes 131104 | tf_op jit(solution)/shard_map/ppermute | solution.py:378
  43.5 0.7 collective-permute-start.8
  44.2 0.9 collective-permute-done.11.refs_1_
  45.2 0.1 multiply_convert_fusion.5.refs_0_
  45.3 0.7 collective-permute-start.9
  46.0 0.7 collective-permute-done.12.refs_0_
  46.7 4.6 %collective-permute-done.9.refs_1_ = bf16[64,1024]{1,0:T(8,128)(2,1)S(1)} collective-permute-done((bf16[64,1024]{1,0:T(8,128)(2,1)S(1)}, bf16[64,1024]{1,0:T(8,128)(2,1)S(1)}, u32[]{:S(2)}, u32[]{:S(2)}) %collective-permute-start.9) | collective-permute-done | bytes 131104 | tf_op jit(solution)/shard_map/ppermute | solution.py:378
  51.4 0.3 shard_map.113
  51.7 0.5 collective-permute-start.14
  52.3 0.7 collective-permute-start.16
  52.9 0.2 collective-permute-done.14
  53.2 0.7 collective-permute-start.17
  53.9 5.2 %collective-permute-done.17.refs_1_ = bf16[64,1024]{1,0:T(8,128)(2,1)S(1)} collective-permute-done((bf16[64,1024]{1,0:T(8,128)(2,1)S(1)}, bf16[64,1024]{1,0:T(8,128)(2,1)S(1)}, u32[]{:S(2)}, u32[]{:S(2)}) %collective-permute-start.17) | collective-permute-done | bytes 131104 | tf_op jit(solution)/shard_map/ppermute | solution.py:378
  59.1 0.7 collective-permute-start.20
  59.8 0.7 collective-permute-start.15
  60.6 1.5 collective-permute-start.21
  62.1 2.8 %collective-permute-done.15.refs_1_ = bf16[64,1024]{1,0:T(8,128)(2,1)S(1)} collective-permute-done((bf16[64,1024]{1,0:T(8,128)(2,1)S(1)}, bf16[64,1024]{1,0:T(8,128)(2,1)S(1)}, u32[]{:S(2)}, u32[]{:S(2)}) %collective-permute-start.15) | collective-permute-done | bytes 131104 | tf_op jit(solution)/shard_map/ppermute | solution.py:378
  64.9 0.7 collective-permute-start.18
  65.9 1.5 collective-permute-start.19
  67.3 4.5 %collective-permute-done.19.refs_1_ = bf16[64,1024]{1,0:T(8,128)(2,1)S(1)} collective-permute-done((bf16[64,1024]{1,0:T(8,128)(2,1)S(1)}, bf16[64,1024]{1,0:T(8,128)(2,1)S(1)}, u32[]{:S(2)}, u32[]{:S(2)}) %collective-permute-start.19) | collective-permute-done | bytes 131104 | tf_op jit(solution)/shard_map/ppermute | solution.py:378
  71.9 1.5 collective-permute-start.24
  73.4 0.7 collective-permute-start.26
  74.1 2.4 %collective-permute-done.24 = f32[64,256]{1,0:T(8,128)S(1)} collective-permute-done((f32[64,256]{1,0:T(8,128)S(1)}, f32[64,256]{1,0:T(8,128)S(1)}, u32[]{:S(2)}, u32[]{:S(2)}) %collective-permute-start.24) | collective-permute-done | bytes 65568 | tf_op jit(solution)/shard_map/ppermute | solution.py:378
  76.5 1.5 collective-permute-start.27
  78.0 3.5 %collective-permute-done.27.refs_1_ = bf16[64,1024]{1,0:T(8,128)(2,1)S(1)} collective-permute-done((bf16[64,1024]{1,0:T(8,128)(2,1)S(1)}, bf16[64,1024]{1,0:T(8,128)(2,1)S(1)}, u32[]{:S(2)}, u32[]{:S(2)}) %collective-permute-start.27) | collective-permute-done | bytes 131104 | tf_op jit(solution)/shard_map/ppermute | solution.py:378
  81.6 1.3 collective-permute-start.30
  82.9 1.5 collective-permute-start.25
  84.4 27.1 %collective-permute-done.30 = bf16[64,1024]{1,0:T(8,128)(2,1)S(1)} collective-permute-done((bf16[64,1024]{1,0:T(8,128)(2,1)S(1)}, bf16[64,1024]{1,0:T(8,128)(2,1)S(1)}, u32[]{:S(2)}, u32[]{:S(2)}) %collective-permute-start.30) | collective-permute-done | bytes 131104 | tf_op jit(solution)/shard_map/ppermute | solution.py:378
  111.6 2.4 %collective-permute-start.31 = (bf16[64,1024]{1,0:T(8,128)(2,1)S(1)}, bf16[64,1024]{1,0:T(8,128)(2,1)S(1)}, u32[]{:S(2)}, u32[]{:S(2)}) collective-permute-start(bf16[64,1024]{1,0:T(8,128)(2,1)S(1)} %multiply_convert_fusion.refs_0_), channel_id=1, source_target_pairs={{0,4},{1,5},{2,6},{3,7},{4,0},{5,1},{6,2},{7,3},{8,12},{9,13},{10,... | collective-permute-start | bytes 393224 | tf_op jit(solution)/shard_map/ppermute | solution.py:378
  114.1 1.3 collective-permute-start.28
  115.4 1.6 %collective-permute-done.31.refs_1_ = bf16[64,1024]{1,0:T(8,128)(2,1)S(1)} collective-permute-done((bf16[64,1024]{1,0:T(8,128)(2,1)S(1)}, bf16[64,1024]{1,0:T(8,128)(2,1)S(1)}, u32[]{:S(2)}, u32[]{:S(2)}) %collective-permute-start.31) | collective-permute-done | bytes 131104 | tf_op jit(solution)/shard_map/ppermute | solution.py:378
  117.0 3.9 %collective-permute-done.28 = bf16[64,1024]{1,0:T(8,128)(2,1)S(1)} collective-permute-done((bf16[64,1024]{1,0:T(8,128)(2,1)S(1)}, bf16[64,1024]{1,0:T(8,128)(2,1)S(1)}, u32[]{:S(2)}, u32[]{:S(2)}) %collective-permute-start.28) | collective-permute-done | bytes 131104 | tf_op jit(solution)/shard_map/ppermute | solution.py:378
  121.0 1.9 %collective-permute-start.29 = (bf16[64,1024]{1,0:T(8,128)(2,1)S(1)}, bf16[64,1024]{1,0:T(8,128)(2,1)S(1)}, u32[]{:S(2)}, u32[]{:S(2)}) collective-permute-start(bf16[64,1024]{1,0:T(8,128)(2,1)S(1)} %multiply_convert_fusion.1.refs_0_), channel_id=1, source_target_pairs={{0,4},{1,5},{2,6},{3,7},{4,0},{5,1},{6,2},{7,3},{8,12},{9,13},{10,... | collective-permute-start | bytes 393224 | tf_op jit(solution)/shard_map/ppermute | solution.py:378
  123.0 1.3 collective-permute-start.34
  124.3 1.3 shard_map.128.refs_2_
  125.6 1.3 shard_map.129.refs_2_
  127.0 4.3 %collective-permute-done.34.refs_3_.refs_4_ = bf16[64,2048]{1,0:T(8,128)(2,1)S(1)} collective-permute-done((bf16[64,2048]{1,0:T(8,128)(2,1)S(1)}, bf16[64,2048]{1,0:T(8,128)(2,1)S(1)}, u32[]{:S(2)}, u32[]{:S(2)}) %collective-permute-start.34) | collective-permute-done | bytes 262176 | tf_op jit(solution)/shard_map/ppermute | solution.py:378
  131.2 0.7 shard_map.132
  132.0 1.1 collective-permute-done.35
  133.2 1.2 shard_map.131.refs_2_
  134.4 0.9 shard_map.133
  135.3 0.9 shard_map.134
  136.2 0.3 collective-permute-start.37
  136.5 1.8 %collective-permute-start.36 = (bf16[64,1024]{1,0:T(8,128)(2,1)S(1)}, bf16[64,1024]{1,0:T(8,128)(2,1)S(1)}, u32[]{:S(2)}, u32[]{:S(2)}) collective-permute-start(bf16[64,1024]{1,0:T(8,128)(2,1)S(1)} %get-tuple-element.50), channel_id=1, source_target_pairs={{0,1},{1,0},{2,3},{3,2},{4,5},{5,4},{6,7},{7,6},{8,9},{9,8},{10,11... | collective-permute-start | bytes 393224 | tf_op jit(solution)/shard_map/ppermute | solution.py:378
  138.3 0.2 collective-permute-start.38
  138.5 3.4 %collective-permute-done.38 = f32[2,16]{1,0:T(2,128)S(1)} collective-permute-done((f32[2,16]{1,0:T(2,128)S(1)}, f32[2,16]{1,0:T(2,128)S(1)}, u32[]{:S(2)}, u32[]{:S(2)}) %collective-permute-start.38) | collective-permute-done | bytes 160 | tf_op jit(solution)/shard_map/ppermute | solution.py:378
  141.9 3.6 %collective-permute-done.39 = f32[2,16]{1,0:T(2,128)S(1)} collective-permute-done((f32[2,16]{1,0:T(2,128)S(1)}, f32[2,16]{1,0:T(2,128)S(1)}, u32[]{:S(2)}, u32[]{:S(2)}) %collective-permute-start.39) | collective-permute-done | bytes 160 | tf_op jit(solution)/shard_map/ppermute | solution.py:378
  145.5 4.5 %collective-permute-done.40 = f32[2,16]{1,0:T(2,128)S(1)} collective-permute-done((f32[2,16]{1,0:T(2,128)S(1)}, f32[2,16]{1,0:T(2,128)S(1)}, u32[]{:S(2)}, u32[]{:S(2)}) %collective-permute-start.40) | collective-permute-done | bytes 160 | tf_op jit(solution)/shard_map/ppermute | solution.py:378
  150.0 0.6 add.39
  150.5 0.9 shard_map.135
  (81 shorter events, 2.0 us)
Async XLA Ops:
  2.1 0.7 collective-permute-start.1
  2.8 13.3 %collective-permute-start.3 = (bf16[64,1024]{1,0:T(8,128)(2,1)S(1)}, bf16[64,1024]{1,0:T(8,128)(2,1)S(1)}, u32[]{:S(2)}, u32[]{:S(2)}) collective-permute-start(bf16[64,1024]{1,0:T(8,128)(2,1)S(1)} %collective-permute-done.1.refs_0_), channel_id=1, source_target_pairs={{0,4},{1,5},{2,6},{3,7},{4,0},{5,1},{6,2},{7,3},{8,12},{9,13},{10,... | collective-permute-start | bytes 393224 | tf_op jit(solution)/shard_map/ppermute | solution.py:378
  16.1 14.4 %collective-permute-start.4 = (bf16[128,1024]{1,0:T(8,128)(2,1)S(1)}, bf16[128,1024]{1,0:T(8,128)(2,1)S(1)}, u32[]{:S(2)}, u32[]{:S(2)}) collective-permute-start(bf16[128,1024]{1,0:T(8,128)(2,1)S(1)} %shard_map.98.refs_0_), channel_id=1, source_target_pairs={{0,2},{1,3},{2,0},{3,1},{4,6},{5,7},{6,4},{7,5},{8,10},{9,11},{10,... | collective-permute-start | bytes 786440 | tf_op jit(solution)/shard_map/ppermute | solution.py:378
  16.1 4.2 %collective-permute-start = (bf16[64,1024]{1,0:T(8,128)(2,1)S(1)}, bf16[64,1024]{1,0:T(8,128)(2,1)S(1)}, u32[]{:S(2)}, u32[]{:S(2)}) collective-permute-start(bf16[64,1024]{1,0:T(8,128)(2,1)S(1)} %get-tuple-element.27), channel_id=1, source_target_pairs={{0,0},{1,4},{2,2},{3,6},{4,1},{5,5},{6,3},{7,7},{8,8},{9,12},{10,1... | collective-permute-start | bytes 393224 | tf_op jit(solution)/shard_map/ppermute | solution.py:378
  20.4 10.1 %collective-permute-start.2 = (bf16[64,1024]{1,0:T(8,128)(2,1)S(1)}, bf16[64,1024]{1,0:T(8,128)(2,1)S(1)}, u32[]{:S(2)}, u32[]{:S(2)}) collective-permute-start(bf16[64,1024]{1,0:T(8,128)(2,1)S(1)} %shard_map.97.refs_0_), channel_id=1, source_target_pairs={{0,4},{1,5},{2,6},{3,7},{4,0},{5,1},{6,2},{7,3},{8,12},{9,13},{10,... | collective-permute-start | bytes 393224 | tf_op jit(solution)/shard_map/ppermute | solution.py:378
  30.6 1.6 %collective-permute-start.5 = (bf16[128,1024]{1,0:T(8,128)(2,1)S(1)}, bf16[128,1024]{1,0:T(8,128)(2,1)S(1)}, u32[]{:S(2)}, u32[]{:S(2)}) collective-permute-start(bf16[128,1024]{1,0:T(8,128)(2,1)S(1)} %shard_map.102.refs_0_), channel_id=1, source_target_pairs={{0,2},{1,3},{2,0},{3,1},{4,6},{5,7},{6,4},{7,5},{8,10},{9,11},{10,... | collective-permute-start | bytes 786440 | tf_op jit(solution)/shard_map/ppermute | solution.py:378
  32.2 5.5 %collective-permute-start.7 = (bf16[64,1024]{1,0:T(8,128)(2,1)S(1)}, bf16[64,1024]{1,0:T(8,128)(2,1)S(1)}, u32[]{:S(2)}, u32[]{:S(2)}) collective-permute-start(bf16[64,1024]{1,0:T(8,128)(2,1)S(1)} %get-tuple-element.33), channel_id=1, source_target_pairs={{0,1},{1,0},{2,3},{3,2},{4,5},{5,4},{6,7},{7,6},{8,9},{9,8},{10,11... | collective-permute-start | bytes 393224 | tf_op jit(solution)/shard_map/ppermute | solution.py:378
  37.8 2.2 %collective-permute-start.10 = (bf16[64,1024]{1,0:T(8,128)(2,1)S(1)}, bf16[64,1024]{1,0:T(8,128)(2,1)S(1)}, u32[]{:S(2)}, u32[]{:S(2)}) collective-permute-start(bf16[64,1024]{1,0:T(8,128)(2,1)S(1)} %shard_map.106.refs_3_), channel_id=1, source_target_pairs={{24,16},{25,20},{26,18},{27,22},{28,17},{29,21},{30,19},{31,23}} | collective-permute-start | bytes 393224 | tf_op jit(solution)/shard_map/ppermute | solution.py:378
  38.5 5.0 %collective-permute-start.6 = (bf16[64,1024]{1,0:T(8,128)(2,1)S(1)}, bf16[64,1024]{1,0:T(8,128)(2,1)S(1)}, u32[]{:S(2)}, u32[]{:S(2)}) collective-permute-start(bf16[64,1024]{1,0:T(8,128)(2,1)S(1)} %get-tuple-element.31), channel_id=1, source_target_pairs={{0,1},{1,0},{2,3},{3,2},{4,5},{5,4},{6,7},{7,6},{8,9},{9,8},{10,11... | collective-permute-start | bytes 393224 | tf_op jit(solution)/shard_map/ppermute | solution.py:378
  40.1 5.0 %collective-permute-start.11 = (bf16[64,1024]{1,0:T(8,128)(2,1)S(1)}, bf16[64,1024]{1,0:T(8,128)(2,1)S(1)}, u32[]{:S(2)}, u32[]{:S(2)}) collective-permute-start(bf16[64,1024]{1,0:T(8,128)(2,1)S(1)} %multiply_convert_fusion.4.refs_0_), channel_id=1, source_target_pairs={{0,4},{1,5},{2,6},{3,7},{4,0},{5,1},{6,2},{7,3},{8,12},{9,13},{10,... | collective-permute-start | bytes 393224 | tf_op jit(solution)/shard_map/ppermute | solution.py:378
  43.5 1.7 %collective-permute-start.8 = (bf16[64,1024]{1,0:T(8,128)(2,1)S(1)}, bf16[64,1024]{1,0:T(8,128)(2,1)S(1)}, u32[]{:S(2)}, u32[]{:S(2)}) collective-permute-start(bf16[64,1024]{1,0:T(8,128)(2,1)S(1)} %get-tuple-element.34), channel_id=1, source_target_pairs={{24,16},{25,20},{26,18},{27,22},{28,17},{29,21},{30,19},{31,23}} | collective-permute-start | bytes 393224 | tf_op jit(solution)/shard_map/ppermute | solution.py:378
  45.1 1.6 %collective-permute-start.12 = (bf16[128,1024]{1,0:T(8,128)(2,1)S(1)}, bf16[128,1024]{1,0:T(8,128)(2,1)S(1)}, u32[]{:S(2)}, u32[]{:S(2)}) collective-permute-start(bf16[128,1024]{1,0:T(8,128)(2,1)S(1)} %shard_map.108.refs_0_), channel_id=1, source_target_pairs={{0,2},{1,3},{2,0},{3,1},{4,6},{5,7},{6,4},{7,5},{8,10},{9,11},{10,... | collective-permute-start | bytes 786440 | tf_op jit(solution)/shard_map/ppermute | solution.py:378
  45.3 6.0 %collective-permute-start.9 = (bf16[64,1024]{1,0:T(8,128)(2,1)S(1)}, bf16[64,1024]{1,0:T(8,128)(2,1)S(1)}, u32[]{:S(2)}, u32[]{:S(2)}) collective-permute-start(bf16[64,1024]{1,0:T(8,128)(2,1)S(1)} %multiply_convert_fusion.5.refs_0_), channel_id=1, source_target_pairs={{0,4},{1,5},{2,6},{3,7},{4,0},{5,1},{6,2},{7,3},{8,12},{9,13},{10,... | collective-permute-start | bytes 393224 | tf_op jit(solution)/shard_map/ppermute | solution.py:378
  46.0 5.4 %copy-start.1 = (bf16[2048,256]{1,0:T(8,128)(2,1)S(1)}, bf16[2048,256]{1,0:T(8,128)(2,1)}, u32[]{:S(2)}) copy-start(bf16[2048,256]{1,0:T(8,128)(2,1)} %factor_ref.1) | copy-start | bytes 3145732
  46.0 5.4 %copy-start.3 = (bf16[64,2048]{1,0:T(8,128)(2,1)S(1)}, bf16[64,2048]{1,0:T(8,128)(2,1)}, u32[]{:S(2)}) copy-start(bf16[64,2048]{1,0:T(8,128)(2,1)} %value_ref.1) | copy-start | bytes 786436
  51.3 1.9 %collective-permute-start.13 = (bf16[128,1024]{1,0:T(8,128)(2,1)S(1)}, bf16[128,1024]{1,0:T(8,128)(2,1)S(1)}, u32[]{:S(2)}, u32[]{:S(2)}) collective-permute-start(bf16[128,1024]{1,0:T(8,128)(2,1)S(1)} %shard_map.111.refs_0_), channel_id=1, source_target_pairs={{0,2},{1,3},{2,0},{3,1},{4,6},{5,7},{6,4},{7,5},{8,10},{9,11},{10,... | collective-permute-start | bytes 786440 | tf_op jit(solution)/shard_map/ppermute | solution.py:378
  51.7 1.4 collective-permute-start.14
  52.3 1.6 %collective-permute-start.16 = (bf16[64,2048]{1,0:T(8,128)(2,1)S(1)}, bf16[64,2048]{1,0:T(8,128)(2,1)S(1)}, u32[]{:S(2)}, u32[]{:S(2)}) collective-permute-start(bf16[64,2048]{1,0:T(8,128)(2,1)S(1)} %get-tuple-element.38.refs_5_), channel_id=1, source_target_pairs={{24,16},{25,17},{26,18},{27,19},{28,20},{29,21},{30,22},{31,23}} | collective-permute-start | bytes 786440 | tf_op jit(solution)/shard_map/ppermute | solution.py:378
  53.2 5.8 %collective-permute-start.17 = (bf16[64,1024]{1,0:T(8,128)(2,1)S(1)}, bf16[64,1024]{1,0:T(8,128)(2,1)S(1)}, u32[]{:S(2)}, u32[]{:S(2)}) collective-permute-start(bf16[64,1024]{1,0:T(8,128)(2,1)S(1)} %get-tuple-element.39), channel_id=1, source_target_pairs={{0,1},{1,0},{2,3},{3,2},{4,5},{5,4},{6,7},{7,6},{8,9},{9,8},{10,11... | collective-permute-start | bytes 393224 | tf_op jit(solution)/shard_map/ppermute | solution.py:378
  59.1 1.4 collective-permute-start.20
  59.8 5.0 %collective-permute-start.15 = (bf16[64,1024]{1,0:T(8,128)(2,1)S(1)}, bf16[64,1024]{1,0:T(8,128)(2,1)S(1)}, u32[]{:S(2)}, u32[]{:S(2)}) collective-permute-start(bf16[64,1024]{1,0:T(8,128)(2,1)S(1)} %get-tuple-element.37), channel_id=1, source_target_pairs={{0,1},{1,0},{2,3},{3,2},{4,5},{5,4},{6,7},{7,6},{8,9},{9,8},{10,11... | collective-permute-start | bytes 393224 | tf_op jit(solution)/shard_map/ppermute | solution.py:378
  60.6 5.0 %collective-permute-start.21 = (bf16[64,1024]{1,0:T(8,128)(2,1)S(1)}, bf16[64,1024]{1,0:T(8,128)(2,1)S(1)}, u32[]{:S(2)}, u32[]{:S(2)}) collective-permute-start(bf16[64,1024]{1,0:T(8,128)(2,1)S(1)} %multiply_convert_fusion.2.refs_0_), channel_id=1, source_target_pairs={{0,4},{1,5},{2,6},{3,7},{4,0},{5,1},{6,2},{7,3},{8,12},{9,13},{10,... | collective-permute-start | bytes 393224 | tf_op jit(solution)/shard_map/ppermute | solution.py:378
  64.9 0.8 collective-permute-start.18
  65.7 1.7 %collective-permute-start.22 = (bf16[128,1024]{1,0:T(8,128)(2,1)S(1)}, bf16[128,1024]{1,0:T(8,128)(2,1)S(1)}, u32[]{:S(2)}, u32[]{:S(2)}) collective-permute-start(bf16[128,1024]{1,0:T(8,128)(2,1)S(1)} %shard_map.118.refs_0_), channel_id=1, source_target_pairs={{0,2},{1,3},{2,0},{3,1},{4,6},{5,7},{6,4},{7,5},{8,10},{9,11},{10,... | collective-permute-start | bytes 786440 | tf_op jit(solution)/shard_map/ppermute | solution.py:378
  65.9 6.0 %collective-permute-start.19 = (bf16[64,1024]{1,0:T(8,128)(2,1)S(1)}, bf16[64,1024]{1,0:T(8,128)(2,1)S(1)}, u32[]{:S(2)}, u32[]{:S(2)}) collective-permute-start(bf16[64,1024]{1,0:T(8,128)(2,1)S(1)} %multiply_convert_fusion.3.refs_0_), channel_id=1, source_target_pairs={{0,4},{1,5},{2,6},{3,7},{4,0},{5,1},{6,2},{7,3},{8,12},{9,13},{10,... | collective-permute-start | bytes 393224 | tf_op jit(solution)/shard_map/ppermute | solution.py:378
  71.8 4.6 %collective-permute-start.23 = (bf16[128,1024]{1,0:T(8,128)(2,1)S(1)}, bf16[128,1024]{1,0:T(8,128)(2,1)S(1)}, u32[]{:S(2)}, u32[]{:S(2)}) collective-permute-start(bf16[128,1024]{1,0:T(8,128)(2,1)S(1)} %shard_map.121.refs_0_), channel_id=1, source_target_pairs={{0,2},{1,3},{2,0},{3,1},{4,6},{5,7},{6,4},{7,5},{8,10},{9,11},{10,... | collective-permute-start | bytes 786440 | tf_op jit(solution)/shard_map/ppermute | solution.py:378
  71.9 4.5 %collective-permute-start.24 = (f32[64,256]{1,0:T(8,128)S(1)}, f32[64,256]{1,0:T(8,128)S(1)}, u32[]{:S(2)}, u32[]{:S(2)}) collective-permute-start(f32[64,256]{1,0:T(8,128)S(1)} %add.34.refs_3_), channel_id=1, source_target_pairs={{0,4},{1,5},{2,6},{3,7},{4,0},{5,1},{6,2},{7,3},{8,12},{9,13},{10,... | collective-permute-start | bytes 196616 | tf_op jit(solution)/shard_map/ppermute | solution.py:378
  73.4 4.6 %collective-permute-start.26 = (bf16[64,2048]{1,0:T(8,128)(2,1)S(1)}, bf16[64,2048]{1,0:T(8,128)(2,1)S(1)}, u32[]{:S(2)}, u32[]{:S(2)}) collective-permute-start(bf16[64,2048]{1,0:T(8,128)(2,1)S(1)} %get-tuple-element.44.refs_6_), channel_id=1, source_target_pairs={{16,8},{17,9},{18,10},{19,11},{20,12},{21,13},{22,14},{23,15}} | collective-permute-start | bytes 786440 | tf_op jit(solution)/shard_map/ppermute | solution.py:378
  76.5 5.0 %collective-permute-start.27 = (bf16[64,1024]{1,0:T(8,128)(2,1)S(1)}, bf16[64,1024]{1,0:T(8,128)(2,1)S(1)}, u32[]{:S(2)}, u32[]{:S(2)}) collective-permute-start(bf16[64,1024]{1,0:T(8,128)(2,1)S(1)} %get-tuple-element.45), channel_id=1, source_target_pairs={{0,1},{1,0},{2,3},{3,2},{4,5},{5,4},{6,7},{7,6},{8,9},{9,8},{10,11... | collective-permute-start | bytes 393224 | tf_op jit(solution)/shard_map/ppermute | solution.py:378
  81.6 29.9 %collective-permute-start.30 = (bf16[64,1024]{1,0:T(8,128)(2,1)S(1)}, bf16[64,1024]{1,0:T(8,128)(2,1)S(1)}, u32[]{:S(2)}, u32[]{:S(2)}) collective-permute-start(bf16[64,1024]{1,0:T(8,128)(2,1)S(1)} %shard_map.125.refs_3_), channel_id=1, source_target_pairs={{8,0},{9,4},{10,2},{11,6},{12,1},{13,5},{14,3},{15,7}} | collective-permute-start | bytes 393224 | tf_op jit(solution)/shard_map/ppermute | solution.py:378
  82.9 31.1 %collective-permute-start.25 = (bf16[64,1024]{1,0:T(8,128)(2,1)S(1)}, bf16[64,1024]{1,0:T(8,128)(2,1)S(1)}, u32[]{:S(2)}, u32[]{:S(2)}) collective-permute-start(bf16[64,1024]{1,0:T(8,128)(2,1)S(1)} %get-tuple-element.43), channel_id=1, source_target_pairs={{0,1},{1,0},{2,3},{3,2},{4,5},{5,4},{6,7},{7,6},{8,9},{9,8},{10,11... | collective-permute-start | bytes 393224 | tf_op jit(solution)/shard_map/ppermute | solution.py:378
  111.6 5.3 %collective-permute-start.31 = (bf16[64,1024]{1,0:T(8,128)(2,1)S(1)}, bf16[64,1024]{1,0:T(8,128)(2,1)S(1)}, u32[]{:S(2)}, u32[]{:S(2)}) collective-permute-start(bf16[64,1024]{1,0:T(8,128)(2,1)S(1)} %multiply_convert_fusion.refs_0_), channel_id=1, source_target_pairs={{0,4},{1,5},{2,6},{3,7},{4,0},{5,1},{6,2},{7,3},{8,12},{9,13},{10,... | collective-permute-start | bytes 393224 | tf_op jit(solution)/shard_map/ppermute | solution.py:378
  114.1 6.9 %collective-permute-start.28 = (bf16[64,1024]{1,0:T(8,128)(2,1)S(1)}, bf16[64,1024]{1,0:T(8,128)(2,1)S(1)}, u32[]{:S(2)}, u32[]{:S(2)}) collective-permute-start(bf16[64,1024]{1,0:T(8,128)(2,1)S(1)} %get-tuple-element.46), channel_id=1, source_target_pairs={{8,0},{9,4},{10,2},{11,6},{12,1},{13,5},{14,3},{15,7}} | collective-permute-start | bytes 393224 | tf_op jit(solution)/shard_map/ppermute | solution.py:378
  117.0 8.6 %collective-permute-start.32 = (bf16[128,1024]{1,0:T(8,128)(2,1)S(1)}, bf16[128,1024]{1,0:T(8,128)(2,1)S(1)}, u32[]{:S(2)}, u32[]{:S(2)}) collective-permute-start(bf16[128,1024]{1,0:T(8,128)(2,1)S(1)} %shard_map.127.refs_0_), channel_id=1, source_target_pairs={{0,2},{1,3},{2,0},{3,1},{4,6},{5,7},{6,4},{7,5},{8,10},{9,11},{10,... | collective-permute-start | bytes 786440 | tf_op jit(solution)/shard_map/ppermute | solution.py:378
  121.0 5.8 %collective-permute-start.29 = (bf16[64,1024]{1,0:T(8,128)(2,1)S(1)}, bf16[64,1024]{1,0:T(8,128)(2,1)S(1)}, u32[]{:S(2)}, u32[]{:S(2)}) collective-permute-start(bf16[64,1024]{1,0:T(8,128)(2,1)S(1)} %multiply_convert_fusion.1.refs_0_), channel_id=1, source_target_pairs={{0,4},{1,5},{2,6},{3,7},{4,0},{5,1},{6,2},{7,3},{8,12},{9,13},{10,... | collective-permute-start | bytes 393224 | tf_op jit(solution)/shard_map/ppermute | solution.py:378
  123.0 8.3 %collective-permute-start.34 = (bf16[64,2048]{1,0:T(8,128)(2,1)S(1)}, bf16[64,2048]{1,0:T(8,128)(2,1)S(1)}, u32[]{:S(2)}, u32[]{:S(2)}) collective-permute-start(bf16[64,2048]{1,0:T(8,128)(2,1)S(1)} %get-tuple-element.47.refs_7_), channel_id=1, source_target_pairs={{8,0},{9,1},{10,2},{11,3},{12,4},{13,5},{14,6},{15,7}} | collective-permute-start | bytes 786440 | tf_op jit(solution)/shard_map/ppermute | solution.py:378
  125.5 5.7 %copy-start = (bf16[2048,256]{1,0:T(8,128)(2,1)S(1)}, bf16[2048,256]{1,0:T(8,128)(2,1)}, u32[]{:S(2)}) copy-start(bf16[2048,256]{1,0:T(8,128)(2,1)} %refs_4_.1) | copy-start | bytes 3145732
  125.5 5.7 %copy-start.2 = (bf16[64,2048]{1,0:T(8,128)(2,1)S(1)}, bf16[64,2048]{1,0:T(8,128)(2,1)}, u32[]{:S(2)}) copy-start(bf16[64,2048]{1,0:T(8,128)(2,1)} %preact_ref.3) | copy-start | bytes 786436
  125.6 5.7 %copy-start.4 = (s32[64]{0:T(128)S(1)}, s32[64]{0:T(128)}, u32[]{:S(2)}) copy-start(s32[64]{0:T(128)} %param.10) | copy-start | bytes 772
  126.9 7.6 %collective-permute-start.33 = (bf16[128,1024]{1,0:T(8,128)(2,1)S(1)}, bf16[128,1024]{1,0:T(8,128)(2,1)S(1)}, u32[]{:S(2)}, u32[]{:S(2)}) collective-permute-start(bf16[128,1024]{1,0:T(8,128)(2,1)S(1)} %shard_map.130.refs_0_), channel_id=1, source_target_pairs={{0,2},{1,3},{2,0},{3,1},{4,6},{5,7},{6,4},{7,5},{8,10},{9,11},{10,... | collective-permute-start | bytes 786440 | tf_op jit(solution)/shard_map/ppermute | solution.py:378
  132.0 1.2 collective-permute-start.35
  136.2 14.3 %collective-permute-start.37 = (bf16[64,1024]{1,0:T(8,128)(2,1)S(1)}, bf16[64,1024]{1,0:T(8,128)(2,1)S(1)}, u32[]{:S(2)}, u32[]{:S(2)}) collective-permute-start(bf16[64,1024]{1,0:T(8,128)(2,1)S(1)} %get-tuple-element.51), channel_id=1, source_target_pairs={{0,1},{1,0},{2,3},{3,2},{4,5},{5,4},{6,7},{7,6},{8,9},{9,8},{10,11... | collective-permute-start | bytes 393224 | tf_op jit(solution)/shard_map/ppermute | solution.py:378
  136.5 14.0 %collective-permute-start.36 = (bf16[64,1024]{1,0:T(8,128)(2,1)S(1)}, bf16[64,1024]{1,0:T(8,128)(2,1)S(1)}, u32[]{:S(2)}, u32[]{:S(2)}) collective-permute-start(bf16[64,1024]{1,0:T(8,128)(2,1)S(1)} %get-tuple-element.50), channel_id=1, source_target_pairs={{0,1},{1,0},{2,3},{3,2},{4,5},{5,4},{6,7},{7,6},{8,9},{9,8},{10,11... | collective-permute-start | bytes 393224 | tf_op jit(solution)/shard_map/ppermute | solution.py:378
  138.3 3.6 %collective-permute-start.38 = (f32[2,16]{1,0:T(2,128)S(1)}, f32[2,16]{1,0:T(2,128)S(1)}, u32[]{:S(2)}, u32[]{:S(2)}) collective-permute-start(f32[2,16]{1,0:T(2,128)S(1)} %add.36.refs_3_), channel_id=1, source_target_pairs={{0,4},{1,5},{2,6},{3,7},{4,0},{5,1},{6,2},{7,3},{8,12},{9,13},{10,... | collective-permute-start | bytes 392 | tf_op jit(solution)/shard_map/ppermute | solution.py:378
  141.9 3.6 %collective-permute-start.39 = (f32[2,16]{1,0:T(2,128)S(1)}, f32[2,16]{1,0:T(2,128)S(1)}, u32[]{:S(2)}, u32[]{:S(2)}) collective-permute-start(f32[2,16]{1,0:T(2,128)S(1)} %add.37), channel_id=1, source_target_pairs={{0,8},{1,9},{2,10},{3,11},{4,12},{5,13},{6,14},{7,15},{8,0},{9,1},... | collective-permute-start | bytes 392 | tf_op jit(solution)/shard_map/ppermute | solution.py:378
  145.5 4.5 %collective-permute-start.40 = (f32[2,16]{1,0:T(2,128)S(1)}, f32[2,16]{1,0:T(2,128)S(1)}, u32[]{:S(2)}, u32[]{:S(2)}) collective-permute-start(f32[2,16]{1,0:T(2,128)S(1)} %add.38), channel_id=1, source_target_pairs={{0,16},{1,17},{2,18},{3,19},{4,20},{5,21},{6,22},{7,23},{8,24},{9,... | collective-permute-start | bytes 392 | tf_op jit(solution)/shard_map/ppermute | solution.py:378

commit v2 on v1

--- a/solution.py
+++ b/solution.py
@@ -71,7 +71,6 @@
 
 def begin(lengths, ids, preacts, cotangent):
     tokens, width = preacts.shape
-    part = width // CHUNKS
     seqs = lengths.shape[0]
 
     def body(length_ref, id_ref, preact_ref, cotangent_ref, *refs):
@@ -104,16 +103,13 @@
         top = (buffer[...].astype(jnp.float32) * scale).astype(jnp.bfloat16)
         top_ref[...] = top
         gate = (slope * top.astype(jnp.float32)).astype(jnp.bfloat16)
-        value = jnp.where(layer == LAYERS - 1, gate, preact)
-        for n in range(CHUNKS):
-            refs[1 + n][...] = value[:, n * part : (n + 1) * part]
-
-    outs = pl.pallas_call(
+        refs[1][...] = jnp.where(layer == LAYERS - 1, gate, preact)
+
+    return pl.pallas_call(
         body,
         in_specs=[HBM, HBM, HBM, HBM],
-        out_specs=[VMEM] * (1 + CHUNKS),
-        out_shape=[jax.ShapeDtypeStruct((tokens, width), jnp.bfloat16)]
-        + [jax.ShapeDtypeStruct((tokens, part), jnp.bfloat16)] * CHUNKS,
+        out_specs=[VMEM] * 2,
+        out_shape=[jax.ShapeDtypeStruct((tokens, width), jnp.bfloat16)] * 2,
         scratch_shapes=[
             pltpu.VMEM((tokens, width), jnp.bfloat16),
             pltpu.SemaphoreType.DMA(()),
@@ -131,7 +127,6 @@
             for value in (lengths, ids, preacts, cotangent)
         ],
     )
-    return outs[0], outs[1:]
 
 
 def product_body(
@@ -233,6 +228,22 @@
     )(*pieces, *after)
 
 
+def gate(grads, preacts, column):
+    rows, width = grads.shape
+
+    def body(grad_ref, preact_ref, out_ref):
+        slope = silu_slope(preact_ref[:, pl.ds(column, width)].astype(jnp.float32))
+        out_ref[...] = (slope * grad_ref[...].astype(jnp.float32)).astype(jnp.bfloat16)
+
+    return pl.pallas_call(
+        body,
+        in_specs=[VMEM, VMEM],
+        out_specs=VMEM,
+        out_shape=jax.ShapeDtypeStruct((rows, width), jnp.bfloat16),
+        compiler_params=small(),
+    )(grads, preacts)
+
+
 def combine(kept, arrived, residual, column, before):
     rows, width = kept.shape
     parts = len(arrived)
@@ -264,7 +275,7 @@
     )(*operands)
 
 
-def finish(parts, arrived, residual, earlier):
+def finish(parts, arrived, residual, earlier, terms):
     rows = residual.shape[0]
     width = parts[0].shape[1]
     count = len(parts)
@@ -272,9 +283,10 @@
 
     def body(*refs):
         layer = spot()[0]
-        out_ref = refs[-1]
+        out_ref, score_ref = refs[-2:]
+        term_refs = refs[-2 - len(terms) : -2]
         residual_ref = refs[count * (1 + per_part)]
-        earlier_refs = refs[count * (1 + per_part) + 1 : -1]
+        earlier_refs = refs[count * (1 + per_part) + 1 : -2 - len(terms)]
         for n in range(count):
             span = pl.ds(n * width, width)
             total = refs[n][...] + residual_ref[:, span].astype(jnp.float32)
@@ -284,16 +296,23 @@
             for tick, ref in enumerate(earlier_refs):
                 value = jnp.where(layer == LAYERS - 1 - tick, ref[:, span], value)
             out_ref[:, span] = value
+        values = [ref[...] for ref in term_refs]
+        while len(values) > 1:
+            values = [values[n] + values[n + 1] for n in range(0, len(values), 2)]
+        score_ref[...] = values[0]
 
     operands = [*parts]
     for group in arrived:
         operands += group
-    operands += [residual, *earlier]
+    operands += [residual, *earlier, *terms]
     return pl.pallas_call(
         body,
         in_specs=[VMEM] * len(operands),
-        out_specs=VMEM,
-        out_shape=jax.ShapeDtypeStruct((rows, width * count), jnp.bfloat16),
+        out_specs=[VMEM, VMEM],
+        out_shape=[
+            jax.ShapeDtypeStruct((rows, width * count), jnp.bfloat16),
+            jax.ShapeDtypeStruct(terms[0].shape, terms[0].dtype),
+        ],
         compiler_params=small(),
     )(*operands)
 
@@ -414,13 +433,9 @@
     id_row = example_ids.reshape(1, tokens)
     top_grad, payload = begin(lengths, id_row, preacts, cotangent)
 
-    turned_payload = [turned(payload[o]) for o in range(CHUNKS)]
-    slope_turned = [silu_slope(value.astype(jnp.float32)) for value in turned_payload]
-    held = [load(weights, 0, cores, [turned_payload[0]])]
-    gates = [turned_payload[0]]
-    for o in range(1, CHUNKS):
-        gates.append(join([turned_payload[o]], [held[o - 1]]))
-        held.append(load(weights, o, cores, [gates[o]]))
+    turned_payload = turned(payload)
+    gates = [turned_payload[:, o * part : (o + 1) * part] for o in range(CHUNKS)]
+    held = [load(weights, o, cores) for o in range(CHUNKS)]
     left_sum = left_side(layer_inputs, query_left)
     residual = top_grad
     candidates = [top_grad]
@@ -455,10 +470,7 @@
                             )
                         )
                 else:
-                    acc = product(
-                        pieces[k], held[o], acc, tick, k, 0, width, groups, cores, False,
-                        held[1:] if tick + o + k == 0 else [],
-                    )
+                    acc = product(pieces[k], held[o], acc, tick, k, 0, width, groups, cores, False)
         arrived = []
         for n in range(CHUNKS):
             arrived.append(
@@ -481,12 +493,14 @@
         gates = []
         for n in range(CHUNKS):
             came = lowered(in_parts[n], tick, True)
-            gates.append((slope_turned[n] * came.astype(jnp.float32)).astype(jnp.bfloat16))
+            gates.append(gate(came, turned_payload, n * part))
         residual = lowered(in_grad, tick, False)
         candidates.append(residual)
 
-    result = finish(kept, arrived, residual, sums)
-    scores = sum_over(terms, "layer", LAYERS)
+    everywhere = [terms]
+    for d in range(1, LAYERS):
+        everywhere.append(send(terms, lambda s, h, k, y: (s ^ d, h, k, y)))
+    result, scores = finish(kept, arrived, residual, sums, everywhere)
     return (result, scores)
 
 

time: 152 us -> 165 us (1.086)
  waiting for transfers between devices: 85.5 us -> 98.2 us
    ppermute x41, waiting for transfers between devices: 85.5 us -> 98.2 us  [send(): return lax.ppermute(value, AXES, pairs)]
  transfers between devices with their start and end apart: 41 -> 41, of which waited for: 22 -> 22; matrix products, arithmetic and copies ran while one was open for 1% -> 0% of each run, Pallas kernels for 8% -> 8%
where the time goes in v2:
time: 165 us
  waiting for transfers between devices  98.2 us (60%)
  starting transfers between devices  48 us (29%)
  Pallas kernels  17.1 us (10%)
    ppermute x41, waiting for transfers between devices, send(): return lax.ppermute(value, AXES, pairs)  98.2 us
    ppermute x41, starting transfers between devices, send(): return lax.ppermute(value, AXES, pairs)  48 us
    pallas_call x2, Pallas kernels, load(): pl.pallas_call(body, in_specs=[HBM] + [ANY] * len(after), out_specs=VMEM,...  7.09 us
    pallas_call x20, Pallas kernels, product(): pl.pallas_call(body, in_specs=specs, out_specs=out_specs, scratch_shapes=...  5.73 us
  transfers between devices with their start and end apart: 41, of which 22 were waited for; matrix products, arithmetic and copies ran while one was open for 0% of the time, Pallas kernels for 8%

profile of v2, /device:TPU:0, one launch (start us, length us, event | category | flops | bytes accessed | tf_op | source)
XLA Modules:
  0.0 164.6 jit_solution(9920895881662154144)
XLA Ops:
  0.6 1.5 shard_map.95
  2.1 0.7 collective-permute-start
  2.8 13.2 %collective-permute-start.2 = (bf16[64,1024]{1,0:T(8,128)(2,1)S(1)}, bf16[64,1024]{1,0:T(8,128)(2,1)S(1)}, u32[]{:S(2)}, u32[]{:S(2)}) collective-permute-start(bf16[64,1024]{1,0:T(8,128)(2,1)S(1)} %get-tuple-element.50.refs_0_), channel_id=1, source_target_pairs={{0,4},{1,5},{2,6},{3,7},{4,0},{5,1},{6,2},{7,3},{8,12},{9,13},{10,... | collective-permute-start | bytes 393224 | tf_op jit(solution)/shard_map/ppermute | solution.py:397
  16.0 2.9 %collective-permute-done.2.refs_1_ = bf16[64,1024]{1,0:T(8,128)(2,1)S(1)} collective-permute-done((bf16[64,1024]{1,0:T(8,128)(2,1)S(1)}, bf16[64,1024]{1,0:T(8,128)(2,1)S(1)}, u32[]{:S(2)}, u32[]{:S(2)}) %collective-permute-start.2) | collective-permute-done | bytes 131104 | tf_op jit(solution)/shard_map/ppermute | solution.py:397
  19.0 2.1 %collective-permute-start.1 = (bf16[64,1024]{1,0:T(8,128)(2,1)S(1)}, bf16[64,1024]{1,0:T(8,128)(2,1)S(1)}, u32[]{:S(2)}, u32[]{:S(2)}) collective-permute-start(bf16[64,1024]{1,0:T(8,128)(2,1)S(1)} %get-tuple-element.51.refs_0_), channel_id=1, source_target_pairs={{0,4},{1,5},{2,6},{3,7},{4,0},{5,1},{6,2},{7,3},{8,12},{9,13},{10,... | collective-permute-start | bytes 393224 | tf_op jit(solution)/shard_map/ppermute | solution.py:397
  21.1 3.5 %shard_map.97.refs_1_ = bf16[2048,2048]{1,0:T(8,128)(2,1)S(1)} custom-call(bf16[2048,4096]{1,0:T(8,128)(2,1)} %weight_ref.3), custom_call_target="tpu_custom_call" | custom-call | tf_op jit(solution)/shard_map/pallas_call | solution.py:62
  24.7 0.5 collective-permute-done.1.refs_1_
  25.3 3.5 %shard_map.101.refs_1_ = bf16[2048,2048]{1,0:T(8,128)(2,1)S(1)} custom-call(bf16[2048,4096]{1,0:T(8,128)(2,1)} %weight_ref.3), custom_call_target="tpu_custom_call" | custom-call | tf_op jit(solution)/shard_map/pallas_call | solution.py:62
  28.9 1.8 %collective-permute-start.6 = (bf16[64,1024]{1,0:T(8,128)(2,1)S(1)}, bf16[64,1024]{1,0:T(8,128)(2,1)S(1)}, u32[]{:S(2)}, u32[]{:S(2)}) collective-permute-start(bf16[64,1024]{1,0:T(8,128)(2,1)S(1)} %get-tuple-element.31), channel_id=1, source_target_pairs={{0,1},{1,0},{2,3},{3,2},{4,5},{5,4},{6,7},{7,6},{8,9},{9,8},{10,11... | collective-permute-start | bytes 393224 | tf_op jit(solution)/shard_map/ppermute | solution.py:397
  30.8 4.2 %collective-permute-done.6.refs_1_ = bf16[64,1024]{1,0:T(8,128)(2,1)S(1)} collective-permute-done((bf16[64,1024]{1,0:T(8,128)(2,1)S(1)}, bf16[64,1024]{1,0:T(8,128)(2,1)S(1)}, u32[]{:S(2)}, u32[]{:S(2)}) %collective-permute-start.6) | collective-permute-done | bytes 131104 | tf_op jit(solution)/shard_map/ppermute | solution.py:397
  35.0 0.7 collective-permute-start.9
  35.8 1.8 %collective-permute-start.10 = (bf16[64,1024]{1,0:T(8,128)(2,1)S(1)}, bf16[64,1024]{1,0:T(8,128)(2,1)S(1)}, u32[]{:S(2)}, u32[]{:S(2)}) collective-permute-start(bf16[64,1024]{1,0:T(8,128)(2,1)S(1)} %shard_map.108.refs_0_), channel_id=1, source_target_pairs={{0,4},{1,5},{2,6},{3,7},{4,0},{5,1},{6,2},{7,3},{8,12},{9,13},{10,... | collective-permute-start | bytes 393224 | tf_op jit(solution)/shard_map/ppermute | solution.py:397
  37.5 0.3 collective-permute-start.5
  37.8 3.0 %collective-permute-done.10.refs_1_ = bf16[64,1024]{1,0:T(8,128)(2,1)S(1)} collective-permute-done((bf16[64,1024]{1,0:T(8,128)(2,1)S(1)}, bf16[64,1024]{1,0:T(8,128)(2,1)S(1)}, u32[]{:S(2)}, u32[]{:S(2)}) %collective-permute-start.10) | collective-permute-done | bytes 131104 | tf_op jit(solution)/shard_map/ppermute | solution.py:397
  41.0 1.5 collective-permute-done.5.refs_1_
  42.6 0.7 collective-permute-start.7
  43.3 0.4 collective-permute-start.8
  43.8 4.6 %collective-permute-done.8.refs_1_ = bf16[64,1024]{1,0:T(8,128)(2,1)S(1)} collective-permute-done((bf16[64,1024]{1,0:T(8,128)(2,1)S(1)}, bf16[64,1024]{1,0:T(8,128)(2,1)S(1)}, u32[]{:S(2)}, u32[]{:S(2)}) %collective-permute-start.8) | collective-permute-done | bytes 131104 | tf_op jit(solution)/shard_map/ppermute | solution.py:397
  48.5 0.3 shard_map.114
  48.8 0.5 collective-permute-start.13
  49.3 0.7 collective-permute-start.15
  50.0 0.2 collective-permute-done.13
  50.3 1.2 collective-permute-start.16
  51.5 4.6 %collective-permute-done.16.refs_1_ = bf16[64,1024]{1,0:T(8,128)(2,1)S(1)} collective-permute-done((bf16[64,1024]{1,0:T(8,128)(2,1)S(1)}, bf16[64,1024]{1,0:T(8,128)(2,1)S(1)}, u32[]{:S(2)}, u32[]{:S(2)}) %collective-permute-start.16) | collective-permute-done | bytes 131104 | tf_op jit(solution)/shard_map/ppermute | solution.py:397
  56.2 0.7 collective-permute-start.19
  56.9 0.1 shard_map.120.refs_0_
  57.0 1.2 collective-permute-start.20
  58.2 1.0 collective-permute-start.14
  59.1 2.9 %collective-permute-done.20.refs_1_ = bf16[64,1024]{1,0:T(8,128)(2,1)S(1)} collective-permute-done((bf16[64,1024]{1,0:T(8,128)(2,1)S(1)}, bf16[64,1024]{1,0:T(8,128)(2,1)S(1)}, u32[]{:S(2)}, u32[]{:S(2)}) %collective-permute-start.20) | collective-permute-done | bytes 131104 | tf_op jit(solution)/shard_map/ppermute | solution.py:397
  62.1 1.0 collective-permute-done.14.refs_1_
  63.2 0.7 collective-permute-start.17
  64.0 1.0 collective-permute-start.18
  65.0 4.0 %collective-permute-done.18.refs_1_ = bf16[64,1024]{1,0:T(8,128)(2,1)S(1)} collective-permute-done((bf16[64,1024]{1,0:T(8,128)(2,1)S(1)}, bf16[64,1024]{1,0:T(8,128)(2,1)S(1)}, u32[]{:S(2)}, u32[]{:S(2)}) %collective-permute-start.18) | collective-permute-done | bytes 131104 | tf_op jit(solution)/shard_map/ppermute | solution.py:397
  69.1 1.1 collective-permute-start.23
  70.2 0.7 collective-permute-start.25
  70.9 2.7 %collective-permute-done.23 = f32[64,256]{1,0:T(8,128)S(1)} collective-permute-done((f32[64,256]{1,0:T(8,128)S(1)}, f32[64,256]{1,0:T(8,128)S(1)}, u32[]{:S(2)}, u32[]{:S(2)}) %collective-permute-start.23) | collective-permute-done | bytes 65568 | tf_op jit(solution)/shard_map/ppermute | solution.py:397
  73.7 1.1 collective-permute-start.26
  74.8 3.9 %collective-permute-done.26.refs_1_ = bf16[64,1024]{1,0:T(8,128)(2,1)S(1)} collective-permute-done((bf16[64,1024]{1,0:T(8,128)(2,1)S(1)}, bf16[64,1024]{1,0:T(8,128)(2,1)S(1)}, u32[]{:S(2)}, u32[]{:S(2)}) %collective-permute-start.26) | collective-permute-done | bytes 131104 | tf_op jit(solution)/shard_map/ppermute | solution.py:397
  78.8 1.3 collective-permute-start.29
  80.1 40.4 %collective-permute-done.29.grad_ref = bf16[64,1024]{1,0:T(8,128)(2,1)S(1)} collective-permute-done((bf16[64,1024]{1,0:T(8,128)(2,1)S(1)}, bf16[64,1024]{1,0:T(8,128)(2,1)S(1)}, u32[]{:S(2)}, u32[]{:S(2)}) %collective-permute-start.29) | collective-permute-done | bytes 131104 | tf_op jit(solution)/shard_map/ppermute | solution.py:397
  120.5 2.3 %collective-permute-start.30 = (bf16[64,1024]{1,0:T(8,128)(2,1)S(1)}, bf16[64,1024]{1,0:T(8,128)(2,1)S(1)}, u32[]{:S(2)}, u32[]{:S(2)}) collective-permute-start(bf16[64,1024]{1,0:T(8,128)(2,1)S(1)} %shard_map.131.refs_0_), channel_id=1, source_target_pairs={{0,4},{1,5},{2,6},{3,7},{4,0},{5,1},{6,2},{7,3},{8,12},{9,13},{10,... | collective-permute-start | bytes 393224 | tf_op jit(solution)/shard_map/ppermute | solution.py:397
  122.8 0.2 collective-permute-start.24
  123.0 2.8 %collective-permute-done.30.refs_1_ = bf16[64,1024]{1,0:T(8,128)(2,1)S(1)} collective-permute-done((bf16[64,1024]{1,0:T(8,128)(2,1)S(1)}, bf16[64,1024]{1,0:T(8,128)(2,1)S(1)}, u32[]{:S(2)}, u32[]{:S(2)}) %collective-permute-start.30) | collective-permute-done | bytes 131104 | tf_op jit(solution)/shard_map/ppermute | solution.py:397
  125.9 1.9 %collective-permute-done.24.refs_1_ = bf16[64,1024]{1,0:T(8,128)(2,1)S(1)} collective-permute-done((bf16[64,1024]{1,0:T(8,128)(2,1)S(1)}, bf16[64,1024]{1,0:T(8,128)(2,1)S(1)}, u32[]{:S(2)}, u32[]{:S(2)}) %collective-permute-start.24) | collective-permute-done | bytes 131104 | tf_op jit(solution)/shard_map/ppermute | solution.py:397
  127.9 1.3 collective-permute-start.27
  129.2 5.6 %collective-permute-done.27.grad_ref = bf16[64,1024]{1,0:T(8,128)(2,1)S(1)} collective-permute-done((bf16[64,1024]{1,0:T(8,128)(2,1)S(1)}, bf16[64,1024]{1,0:T(8,128)(2,1)S(1)}, u32[]{:S(2)}, u32[]{:S(2)}) %collective-permute-start.27) | collective-permute-done | bytes 131104 | tf_op jit(solution)/shard_map/ppermute | solution.py:397
  134.8 2.9 %collective-permute-start.28 = (bf16[64,1024]{1,0:T(8,128)(2,1)S(1)}, bf16[64,1024]{1,0:T(8,128)(2,1)S(1)}, u32[]{:S(2)}, u32[]{:S(2)}) collective-permute-start(bf16[64,1024]{1,0:T(8,128)(2,1)S(1)} %shard_map.130.refs_0_), channel_id=1, source_target_pairs={{0,4},{1,5},{2,6},{3,7},{4,0},{5,1},{6,2},{7,3},{8,12},{9,13},{10,... | collective-permute-start | bytes 393224 | tf_op jit(solution)/shard_map/ppermute | solution.py:397
  137.7 1.3 collective-permute-start.33
  139.0 1.3 shard_map.133.refs_2_
  140.3 1.3 shard_map.134.refs_2_
  141.7 5.5 %collective-permute-done.33.refs_3_.refs_4_ = bf16[64,2048]{1,0:T(8,128)(2,1)S(1)} collective-permute-done((bf16[64,2048]{1,0:T(8,128)(2,1)S(1)}, bf16[64,2048]{1,0:T(8,128)(2,1)S(1)}, u32[]{:S(2)}, u32[]{:S(2)}) %collective-permute-start.33) | collective-permute-done | bytes 262176 | tf_op jit(solution)/shard_map/ppermute | solution.py:397
  147.2 0.7 shard_map.137
  147.9 1.1 collective-permute-done.34
  149.1 1.2 shard_map.136.refs_2_
  150.3 0.9 shard_map.138
  151.2 0.9 shard_map.139
  152.1 0.5 collective-permute-start.36
  152.6 1.6 collective-permute-start.35
  154.2 0.4 collective-permute-start.37
  154.6 3.2 %collective-permute-done.37 = f32[2,16]{1,0:T(2,128)S(1)} collective-permute-done((f32[2,16]{1,0:T(2,128)S(1)}, f32[2,16]{1,0:T(2,128)S(1)}, u32[]{:S(2)}, u32[]{:S(2)}) %collective-permute-start.37) | collective-permute-done | bytes 160 | tf_op jit(solution)/shard_map/ppermute | solution.py:397
  157.8 4.4 %collective-permute-start.38 = (f32[2,16]{1,0:T(2,128)S(1)}, f32[2,16]{1,0:T(2,128)S(1)}, u32[]{:S(2)}, u32[]{:S(2)}) collective-permute-start(f32[2,16]{1,0:T(2,128)S(1)} %add.15.refs_8_), channel_id=1, source_target_pairs={{0,8},{1,9},{2,10},{3,11},{4,12},{5,13},{6,14},{7,15},{8,0},{9,1},... | collective-permute-start | bytes 392 | tf_op jit(solution)/shard_map/ppermute | solution.py:397
  162.2 1.0 collective-permute-done.40.refs_11_
  163.2 0.6 collective-permute-done.38.refs_9_
  163.8 0.8 shard_map.140
  (79 shorter events, 1.8 us)
Async XLA Ops:
  2.1 0.7 collective-permute-start
  2.8 16.1 %collective-permute-start.2 = (bf16[64,1024]{1,0:T(8,128)(2,1)S(1)}, bf16[64,1024]{1,0:T(8,128)(2,1)S(1)}, u32[]{:S(2)}, u32[]{:S(2)}) collective-permute-start(bf16[64,1024]{1,0:T(8,128)(2,1)S(1)} %get-tuple-element.50.refs_0_), channel_id=1, source_target_pairs={{0,4},{1,5},{2,6},{3,7},{4,0},{5,1},{6,2},{7,3},{8,12},{9,13},{10,... | collective-permute-start | bytes 393224 | tf_op jit(solution)/shard_map/ppermute | solution.py:397
  19.0 5.7 %collective-permute-start.3 = (bf16[128,1024]{1,0:T(8,128)(2,1)S(1)}, bf16[128,1024]{1,0:T(8,128)(2,1)S(1)}, u32[]{:S(2)}, u32[]{:S(2)}) collective-permute-start(bf16[128,1024]{1,0:T(8,128)(2,1)S(1)} %shard_map.96.refs_0_), channel_id=1, source_target_pairs={{0,2},{1,3},{2,0},{3,1},{4,6},{5,7},{6,4},{7,5},{8,10},{9,11},{10,... | collective-permute-start | bytes 786440 | tf_op jit(solution)/shard_map/ppermute | solution.py:397
  19.0 6.2 %collective-permute-start.1 = (bf16[64,1024]{1,0:T(8,128)(2,1)S(1)}, bf16[64,1024]{1,0:T(8,128)(2,1)S(1)}, u32[]{:S(2)}, u32[]{:S(2)}) collective-permute-start(bf16[64,1024]{1,0:T(8,128)(2,1)S(1)} %get-tuple-element.51.refs_0_), channel_id=1, source_target_pairs={{0,4},{1,5},{2,6},{3,7},{4,0},{5,1},{6,2},{7,3},{8,12},{9,13},{10,... | collective-permute-start | bytes 393224 | tf_op jit(solution)/shard_map/ppermute | solution.py:397
  25.2 3.7 %collective-permute-start.4 = (bf16[128,1024]{1,0:T(8,128)(2,1)S(1)}, bf16[128,1024]{1,0:T(8,128)(2,1)S(1)}, u32[]{:S(2)}, u32[]{:S(2)}) collective-permute-start(bf16[128,1024]{1,0:T(8,128)(2,1)S(1)} %shard_map.100.refs_0_), channel_id=1, source_target_pairs={{0,2},{1,3},{2,0},{3,1},{4,6},{5,7},{6,4},{7,5},{8,10},{9,11},{10,... | collective-permute-start | bytes 786440 | tf_op jit(solution)/shard_map/ppermute | solution.py:397
  28.9 6.0 %collective-permute-start.6 = (bf16[64,1024]{1,0:T(8,128)(2,1)S(1)}, bf16[64,1024]{1,0:T(8,128)(2,1)S(1)}, u32[]{:S(2)}, u32[]{:S(2)}) collective-permute-start(bf16[64,1024]{1,0:T(8,128)(2,1)S(1)} %get-tuple-element.31), channel_id=1, source_target_pairs={{0,1},{1,0},{2,3},{3,2},{4,5},{5,4},{6,7},{7,6},{8,9},{9,8},{10,11... | collective-permute-start | bytes 393224 | tf_op jit(solution)/shard_map/ppermute | solution.py:397
  35.0 0.7 collective-permute-start.9
  35.8 5.1 %collective-permute-start.10 = (bf16[64,1024]{1,0:T(8,128)(2,1)S(1)}, bf16[64,1024]{1,0:T(8,128)(2,1)S(1)}, u32[]{:S(2)}, u32[]{:S(2)}) collective-permute-start(bf16[64,1024]{1,0:T(8,128)(2,1)S(1)} %shard_map.108.refs_0_), channel_id=1, source_target_pairs={{0,4},{1,5},{2,6},{3,7},{4,0},{5,1},{6,2},{7,3},{8,12},{9,13},{10,... | collective-permute-start | bytes 393224 | tf_op jit(solution)/shard_map/ppermute | solution.py:397
  37.5 5.0 %collective-permute-start.5 = (bf16[64,1024]{1,0:T(8,128)(2,1)S(1)}, bf16[64,1024]{1,0:T(8,128)(2,1)S(1)}, u32[]{:S(2)}, u32[]{:S(2)}) collective-permute-start(bf16[64,1024]{1,0:T(8,128)(2,1)S(1)} %get-tuple-element.29), channel_id=1, source_target_pairs={{0,1},{1,0},{2,3},{3,2},{4,5},{5,4},{6,7},{7,6},{8,9},{9,8},{10,11... | collective-permute-start | bytes 393224 | tf_op jit(solution)/shard_map/ppermute | solution.py:397
  40.9 2.8 %collective-permute-start.11 = (bf16[128,1024]{1,0:T(8,128)(2,1)S(1)}, bf16[128,1024]{1,0:T(8,128)(2,1)S(1)}, u32[]{:S(2)}, u32[]{:S(2)}) collective-permute-start(bf16[128,1024]{1,0:T(8,128)(2,1)S(1)} %shard_map.109.refs_0_), channel_id=1, source_target_pairs={{0,2},{1,3},{2,0},{3,1},{4,6},{5,7},{6,4},{7,5},{8,10},{9,11},{10,... | collective-permute-start | bytes 786440 | tf_op jit(solution)/shard_map/ppermute | solution.py:397
  42.6 0.7 collective-permute-start.7
  43.3 5.0 %collective-permute-start.8 = (bf16[64,1024]{1,0:T(8,128)(2,1)S(1)}, bf16[64,1024]{1,0:T(8,128)(2,1)S(1)}, u32[]{:S(2)}, u32[]{:S(2)}) collective-permute-start(bf16[64,1024]{1,0:T(8,128)(2,1)S(1)} %shard_map.107.refs_0_), channel_id=1, source_target_pairs={{0,4},{1,5},{2,6},{3,7},{4,0},{5,1},{6,2},{7,3},{8,12},{9,13},{10,... | collective-permute-start | bytes 393224 | tf_op jit(solution)/shard_map/ppermute | solution.py:397
  43.7 4.8 %copy-start.1 = (bf16[2048,256]{1,0:T(8,128)(2,1)S(1)}, bf16[2048,256]{1,0:T(8,128)(2,1)}, u32[]{:S(2)}) copy-start(bf16[2048,256]{1,0:T(8,128)(2,1)} %factor_ref.1) | copy-start | bytes 3145732
  43.7 4.8 %copy-start.3 = (bf16[64,2048]{1,0:T(8,128)(2,1)S(1)}, bf16[64,2048]{1,0:T(8,128)(2,1)}, u32[]{:S(2)}) copy-start(bf16[64,2048]{1,0:T(8,128)(2,1)} %value_ref.1) | copy-start | bytes 786436
  48.4 1.9 %collective-permute-start.12 = (bf16[128,1024]{1,0:T(8,128)(2,1)S(1)}, bf16[128,1024]{1,0:T(8,128)(2,1)S(1)}, u32[]{:S(2)}, u32[]{:S(2)}) collective-permute-start(bf16[128,1024]{1,0:T(8,128)(2,1)S(1)} %shard_map.112.refs_0_), channel_id=1, source_target_pairs={{0,2},{1,3},{2,0},{3,1},{4,6},{5,7},{6,4},{7,5},{8,10},{9,11},{10,... | collective-permute-start | bytes 786440 | tf_op jit(solution)/shard_map/ppermute | solution.py:397
  48.8 1.5 collective-permute-start.13
  49.3 2.2 %collective-permute-start.15 = (bf16[64,2048]{1,0:T(8,128)(2,1)S(1)}, bf16[64,2048]{1,0:T(8,128)(2,1)S(1)}, u32[]{:S(2)}, u32[]{:S(2)}) collective-permute-start(bf16[64,2048]{1,0:T(8,128)(2,1)S(1)} %get-tuple-element.36.refs_5_), channel_id=1, source_target_pairs={{24,16},{25,17},{26,18},{27,19},{28,20},{29,21},{30,22},{31,23}} | collective-permute-start | bytes 786440 | tf_op jit(solution)/shard_map/ppermute | solution.py:397
  50.3 5.8 %collective-permute-start.16 = (bf16[64,1024]{1,0:T(8,128)(2,1)S(1)}, bf16[64,1024]{1,0:T(8,128)(2,1)S(1)}, u32[]{:S(2)}, u32[]{:S(2)}) collective-permute-start(bf16[64,1024]{1,0:T(8,128)(2,1)S(1)} %get-tuple-element.37), channel_id=1, source_target_pairs={{0,1},{1,0},{2,3},{3,2},{4,5},{5,4},{6,7},{7,6},{8,9},{9,8},{10,11... | collective-permute-start | bytes 393224 | tf_op jit(solution)/shard_map/ppermute | solution.py:397
  56.2 0.7 collective-permute-start.19
  57.0 5.0 %collective-permute-start.20 = (bf16[64,1024]{1,0:T(8,128)(2,1)S(1)}, bf16[64,1024]{1,0:T(8,128)(2,1)S(1)}, u32[]{:S(2)}, u32[]{:S(2)}) collective-permute-start(bf16[64,1024]{1,0:T(8,128)(2,1)S(1)} %shard_map.120.refs_0_), channel_id=1, source_target_pairs={{0,4},{1,5},{2,6},{3,7},{4,0},{5,1},{6,2},{7,3},{8,12},{9,13},{10,... | collective-permute-start | bytes 393224 | tf_op jit(solution)/shard_map/ppermute | solution.py:397
  58.2 5.0 %collective-permute-start.14 = (bf16[64,1024]{1,0:T(8,128)(2,1)S(1)}, bf16[64,1024]{1,0:T(8,128)(2,1)S(1)}, u32[]{:S(2)}, u32[]{:S(2)}) collective-permute-start(bf16[64,1024]{1,0:T(8,128)(2,1)S(1)} %get-tuple-element.35), channel_id=1, source_target_pairs={{0,1},{1,0},{2,3},{3,2},{4,5},{5,4},{6,7},{7,6},{8,9},{9,8},{10,11... | collective-permute-start | bytes 393224 | tf_op jit(solution)/shard_map/ppermute | solution.py:397
  62.0 2.9 %collective-permute-start.21 = (bf16[128,1024]{1,0:T(8,128)(2,1)S(1)}, bf16[128,1024]{1,0:T(8,128)(2,1)S(1)}, u32[]{:S(2)}, u32[]{:S(2)}) collective-permute-start(bf16[128,1024]{1,0:T(8,128)(2,1)S(1)} %shard_map.121.refs_0_), channel_id=1, source_target_pairs={{0,2},{1,3},{2,0},{3,1},{4,6},{5,7},{6,4},{7,5},{8,10},{9,11},{10,... | collective-permute-start | bytes 786440 | tf_op jit(solution)/shard_map/ppermute | solution.py:397
  63.2 0.7 collective-permute-start.17
  64.0 5.0 %collective-permute-start.18 = (bf16[64,1024]{1,0:T(8,128)(2,1)S(1)}, bf16[64,1024]{1,0:T(8,128)(2,1)S(1)}, u32[]{:S(2)}, u32[]{:S(2)}) collective-permute-start(bf16[64,1024]{1,0:T(8,128)(2,1)S(1)} %shard_map.119.refs_0_), channel_id=1, source_target_pairs={{0,4},{1,5},{2,6},{3,7},{4,0},{5,1},{6,2},{7,3},{8,12},{9,13},{10,... | collective-permute-start | bytes 393224 | tf_op jit(solution)/shard_map/ppermute | solution.py:397
  69.0 4.6 %collective-permute-start.22 = (bf16[128,1024]{1,0:T(8,128)(2,1)S(1)}, bf16[128,1024]{1,0:T(8,128)(2,1)S(1)}, u32[]{:S(2)}, u32[]{:S(2)}) collective-permute-start(bf16[128,1024]{1,0:T(8,128)(2,1)S(1)} %shard_map.124.refs_0_), channel_id=1, source_target_pairs={{0,2},{1,3},{2,0},{3,1},{4,6},{5,7},{6,4},{7,5},{8,10},{9,11},{10,... | collective-permute-start | bytes 786440 | tf_op jit(solution)/shard_map/ppermute | solution.py:397
  69.1 4.5 %collective-permute-start.23 = (f32[64,256]{1,0:T(8,128)S(1)}, f32[64,256]{1,0:T(8,128)S(1)}, u32[]{:S(2)}, u32[]{:S(2)}) collective-permute-start(f32[64,256]{1,0:T(8,128)S(1)} %add.12.refs_3_), channel_id=1, source_target_pairs={{0,4},{1,5},{2,6},{3,7},{4,0},{5,1},{6,2},{7,3},{8,12},{9,13},{10,... | collective-permute-start | bytes 196616 | tf_op jit(solution)/shard_map/ppermute | solution.py:397
  70.2 4.6 %collective-permute-start.25 = (bf16[64,2048]{1,0:T(8,128)(2,1)S(1)}, bf16[64,2048]{1,0:T(8,128)(2,1)S(1)}, u32[]{:S(2)}, u32[]{:S(2)}) collective-permute-start(bf16[64,2048]{1,0:T(8,128)(2,1)S(1)} %get-tuple-element.42.refs_6_), channel_id=1, source_target_pairs={{16,8},{17,9},{18,10},{19,11},{20,12},{21,13},{22,14},{23,15}} | collective-permute-start | bytes 786440 | tf_op jit(solution)/shard_map/ppermute | solution.py:397
  73.7 5.0 %collective-permute-start.26 = (bf16[64,1024]{1,0:T(8,128)(2,1)S(1)}, bf16[64,1024]{1,0:T(8,128)(2,1)S(1)}, u32[]{:S(2)}, u32[]{:S(2)}) collective-permute-start(bf16[64,1024]{1,0:T(8,128)(2,1)S(1)} %get-tuple-element.43), channel_id=1, source_target_pairs={{0,1},{1,0},{2,3},{3,2},{4,5},{5,4},{6,7},{7,6},{8,9},{9,8},{10,11... | collective-permute-start | bytes 393224 | tf_op jit(solution)/shard_map/ppermute | solution.py:397
  78.8 41.7 %collective-permute-start.29 = (bf16[64,1024]{1,0:T(8,128)(2,1)S(1)}, bf16[64,1024]{1,0:T(8,128)(2,1)S(1)}, u32[]{:S(2)}, u32[]{:S(2)}) collective-permute-start(bf16[64,1024]{1,0:T(8,128)(2,1)S(1)} %shard_map.128.refs_3_), channel_id=1, source_target_pairs={{8,0},{9,4},{10,2},{11,6},{12,1},{13,5},{14,3},{15,7}} | collective-permute-start | bytes 393224 | tf_op jit(solution)/shard_map/ppermute | solution.py:397
  120.5 5.3 %collective-permute-start.30 = (bf16[64,1024]{1,0:T(8,128)(2,1)S(1)}, bf16[64,1024]{1,0:T(8,128)(2,1)S(1)}, u32[]{:S(2)}, u32[]{:S(2)}) collective-permute-start(bf16[64,1024]{1,0:T(8,128)(2,1)S(1)} %shard_map.131.refs_0_), channel_id=1, source_target_pairs={{0,4},{1,5},{2,6},{3,7},{4,0},{5,1},{6,2},{7,3},{8,12},{9,13},{10,... | collective-permute-start | bytes 393224 | tf_op jit(solution)/shard_map/ppermute | solution.py:397
  122.8 5.0 %collective-permute-start.24 = (bf16[64,1024]{1,0:T(8,128)(2,1)S(1)}, bf16[64,1024]{1,0:T(8,128)(2,1)S(1)}, u32[]{:S(2)}, u32[]{:S(2)}) collective-permute-start(bf16[64,1024]{1,0:T(8,128)(2,1)S(1)} %get-tuple-element.41), channel_id=1, source_target_pairs={{0,1},{1,0},{2,3},{3,2},{4,5},{5,4},{6,7},{7,6},{8,9},{9,8},{10,11... | collective-permute-start | bytes 393224 | tf_op jit(solution)/shard_map/ppermute | solution.py:397
  125.8 14.5 %collective-permute-start.31 = (bf16[128,1024]{1,0:T(8,128)(2,1)S(1)}, bf16[128,1024]{1,0:T(8,128)(2,1)S(1)}, u32[]{:S(2)}, u32[]{:S(2)}) collective-permute-start(bf16[128,1024]{1,0:T(8,128)(2,1)S(1)} %shard_map.132.refs_0_), channel_id=1, source_target_pairs={{0,2},{1,3},{2,0},{3,1},{4,6},{5,7},{6,4},{7,5},{8,10},{9,11},{10,... | collective-permute-start | bytes 786440 | tf_op jit(solution)/shard_map/ppermute | solution.py:397
  127.9 6.9 %collective-permute-start.27 = (bf16[64,1024]{1,0:T(8,128)(2,1)S(1)}, bf16[64,1024]{1,0:T(8,128)(2,1)S(1)}, u32[]{:S(2)}, u32[]{:S(2)}) collective-permute-start(bf16[64,1024]{1,0:T(8,128)(2,1)S(1)} %get-tuple-element.44), channel_id=1, source_target_pairs={{8,0},{9,4},{10,2},{11,6},{12,1},{13,5},{14,3},{15,7}} | collective-permute-start | bytes 393224 | tf_op jit(solution)/shard_map/ppermute | solution.py:397
  134.8 6.8 %collective-permute-start.28 = (bf16[64,1024]{1,0:T(8,128)(2,1)S(1)}, bf16[64,1024]{1,0:T(8,128)(2,1)S(1)}, u32[]{:S(2)}, u32[]{:S(2)}) collective-permute-start(bf16[64,1024]{1,0:T(8,128)(2,1)S(1)} %shard_map.130.refs_0_), channel_id=1, source_target_pairs={{0,4},{1,5},{2,6},{3,7},{4,0},{5,1},{6,2},{7,3},{8,12},{9,13},{10,... | collective-permute-start | bytes 393224 | tf_op jit(solution)/shard_map/ppermute | solution.py:397
  137.7 9.4 %collective-permute-start.33 = (bf16[64,2048]{1,0:T(8,128)(2,1)S(1)}, bf16[64,2048]{1,0:T(8,128)(2,1)S(1)}, u32[]{:S(2)}, u32[]{:S(2)}) collective-permute-start(bf16[64,2048]{1,0:T(8,128)(2,1)S(1)} %get-tuple-element.45.refs_7_), channel_id=1, source_target_pairs={{8,0},{9,1},{10,2},{11,3},{12,4},{13,5},{14,6},{15,7}} | collective-permute-start | bytes 786440 | tf_op jit(solution)/shard_map/ppermute | solution.py:397
  140.3 6.9 %copy-start = (bf16[2048,256]{1,0:T(8,128)(2,1)S(1)}, bf16[2048,256]{1,0:T(8,128)(2,1)}, u32[]{:S(2)}) copy-start(bf16[2048,256]{1,0:T(8,128)(2,1)} %refs_4_.1) | copy-start | bytes 3145732
  140.3 6.9 %copy-start.2 = (bf16[64,2048]{1,0:T(8,128)(2,1)S(1)}, bf16[64,2048]{1,0:T(8,128)(2,1)}, u32[]{:S(2)}) copy-start(bf16[64,2048]{1,0:T(8,128)(2,1)} %preact_ref.3) | copy-start | bytes 786436
  140.3 6.9 %copy-start.4 = (s32[64]{0:T(128)S(1)}, s32[64]{0:T(128)}, u32[]{:S(2)}) copy-start(s32[64]{0:T(128)} %param.10) | copy-start | bytes 772
  141.6 8.7 %collective-permute-start.32 = (bf16[128,1024]{1,0:T(8,128)(2,1)S(1)}, bf16[128,1024]{1,0:T(8,128)(2,1)S(1)}, u32[]{:S(2)}, u32[]{:S(2)}) collective-permute-start(bf16[128,1024]{1,0:T(8,128)(2,1)S(1)} %shard_map.135.refs_0_), channel_id=1, source_target_pairs={{0,2},{1,3},{2,0},{3,1},{4,6},{5,7},{6,4},{7,5},{8,10},{9,11},{10,... | collective-permute-start | bytes 786440 | tf_op jit(solution)/shard_map/ppermute | solution.py:397
  147.9 1.2 collective-permute-start.34
  152.1 11.6 %collective-permute-start.36 = (bf16[64,1024]{1,0:T(8,128)(2,1)S(1)}, bf16[64,1024]{1,0:T(8,128)(2,1)S(1)}, u32[]{:S(2)}, u32[]{:S(2)}) collective-permute-start(bf16[64,1024]{1,0:T(8,128)(2,1)S(1)} %get-tuple-element.49), channel_id=1, source_target_pairs={{0,1},{1,0},{2,3},{3,2},{4,5},{5,4},{6,7},{7,6},{8,9},{9,8},{10,11... | collective-permute-start | bytes 393224 | tf_op jit(solution)/shard_map/ppermute | solution.py:397
  152.6 11.1 %collective-permute-start.35 = (bf16[64,1024]{1,0:T(8,128)(2,1)S(1)}, bf16[64,1024]{1,0:T(8,128)(2,1)S(1)}, u32[]{:S(2)}, u32[]{:S(2)}) collective-permute-start(bf16[64,1024]{1,0:T(8,128)(2,1)S(1)} %get-tuple-element.48), channel_id=1, source_target_pairs={{0,1},{1,0},{2,3},{3,2},{4,5},{5,4},{6,7},{7,6},{8,9},{9,8},{10,11... | collective-permute-start | bytes 393224 | tf_op jit(solution)/shard_map/ppermute | solution.py:397
  154.2 3.6 %collective-permute-start.37 = (f32[2,16]{1,0:T(2,128)S(1)}, f32[2,16]{1,0:T(2,128)S(1)}, u32[]{:S(2)}, u32[]{:S(2)}) collective-permute-start(f32[2,16]{1,0:T(2,128)S(1)} %add.14.refs_3_), channel_id=1, source_target_pairs={{0,4},{1,5},{2,6},{3,7},{4,0},{5,1},{6,2},{7,3},{8,12},{9,13},{10,... | collective-permute-start | bytes 392 | tf_op jit(solution)/shard_map/ppermute | solution.py:397
  157.8 5.4 %collective-permute-start.40 = (f32[2,16]{1,0:T(2,128)S(1)}, f32[2,16]{1,0:T(2,128)S(1)}, u32[]{:S(2)}, u32[]{:S(2)}) collective-permute-start(f32[2,16]{1,0:T(2,128)S(1)} %add.15.refs_8_), channel_id=1, source_target_pairs={{0,24},{1,25},{2,26},{3,27},{4,28},{5,29},{6,30},{7,31},{8,16},{9,... | collective-permute-start | bytes 392 | tf_op jit(solution)/shard_map/ppermute | solution.py:397
  157.8 5.4 %collective-permute-start.39 = (f32[2,16]{1,0:T(2,128)S(1)}, f32[2,16]{1,0:T(2,128)S(1)}, u32[]{:S(2)}, u32[]{:S(2)}) collective-permute-start(f32[2,16]{1,0:T(2,128)S(1)} %add.15.refs_8_), channel_id=1, source_target_pairs={{0,16},{1,17},{2,18},{3,19},{4,20},{5,21},{6,22},{7,23},{8,24},{9,... | collective-permute-start | bytes 392 | tf_op jit(solution)/shard_map/ppermute | solution.py:397
  157.8 5.9 %collective-permute-start.38 = (f32[2,16]{1,0:T(2,128)S(1)}, f32[2,16]{1,0:T(2,128)S(1)}, u32[]{:S(2)}, u32[]{:S(2)}) collective-permute-start(f32[2,16]{1,0:T(2,128)S(1)} %add.15.refs_8_), channel_id=1, source_target_pairs={{0,8},{1,9},{2,10},{3,11},{4,12},{5,13},{6,14},{7,15},{8,0},{9,1},... | collective-permute-start | bytes 392 | tf_op jit(solution)/shard_map/ppermute | solution.py:397

commit v3 on v2

--- a/solution.py
+++ b/solution.py
@@ -212,12 +212,12 @@
     )(*operands)
 
 
-def join(pieces, after):
-    rows, width = pieces[0].shape
+def join(pieces, column, width, after):
+    rows = pieces[0].shape[0]
 
     def body(*refs):
         for n in range(len(pieces)):
-            refs[-1][pl.ds(n * rows, rows), :] = refs[n][...]
+            refs[-1][pl.ds(n * rows, rows), :] = refs[n][:, pl.ds(column, width)]
 
     return pl.pallas_call(
         body,
@@ -434,7 +434,10 @@
     top_grad, payload = begin(lengths, id_row, preacts, cotangent)
 
     turned_payload = turned(payload)
-    gates = [turned_payload[:, o * part : (o + 1) * part] for o in range(CHUNKS)]
+    crossed = [
+        send(payload, lambda s, h, k, y: (s, (y - d) % groups, k, h))
+        for d in range(1, groups)
+    ]
     held = [load(weights, o, cores) for o in range(CHUNKS)]
     left_sum = left_side(layer_inputs, query_left)
     residual = top_grad
@@ -444,7 +447,10 @@
         last = tick == LAYERS - 1
         acc = None
         parts = []
-        mine_sent = [from_places(gates[o]) for o in range(CHUNKS)]
+        if tick == 0:
+            owned = [[turned_payload] + crossed] * CHUNKS
+        else:
+            owned = [[gates[o]] + from_places(gates[o]) for o in range(CHUNKS)]
         behind = []
         if tick == 1:
             left_sum = sum_over(left_sum, "core", cores)
@@ -455,10 +461,11 @@
         if last:
             terms = score_terms(id_row, preacts, candidates, query_right, left_sum, seqs)
             terms = sum_over(terms, "core", cores)
-            behind = [terms]
             terms = sum_over(terms, "place", groups)
         for o in range(CHUNKS):
-            mine = join([gates[o]] + mine_sent[o], [] if acc is None else [acc])
+            column = o * part if tick == 0 else 0
+            behind_join = [acc] if tick and o else []
+            mine = join(owned[o], column, part, behind_join)
             pieces = [mine] + from_cores(mine)
             for k in range(cores):
                 if o == CHUNKS - 1 and k == cores - 1:

time: 165 us -> 159 us (0.964)
  starting transfers between devices: 48 us -> 40.7 us
    ppermute x41 -> x40, starting transfers between devices: 48 us -> 40.7 us  [send(): return lax.ppermute(value, AXES, pairs)]
    ppermute x41 -> x40, waiting for transfers between devices: 98.2 us -> 99.5 us  [send(): return lax.ppermute(value, AXES, pairs)]
  transfers between devices with their start and end apart: 41 -> 40, of which waited for: 22 -> 22; matrix products, arithmetic and copies ran while one was open for 0% -> 0% of each run, Pallas kernels for 8% -> 9%
where the time goes in v3:
time: 159 us; the launch traced here: 158 us
  waiting for transfers between devices  99.5 us (63%)
  starting transfers between devices  40.7 us (26%)
  Pallas kernels  17.1 us (11%)
    ppermute x40, waiting for transfers between devices, send(): return lax.ppermute(value, AXES, pairs)  99.5 us
    ppermute x40, starting transfers between devices, send(): return lax.ppermute(value, AXES, pairs)  40.7 us
    pallas_call x2, Pallas kernels, load(): pl.pallas_call(body, in_specs=[HBM] + [ANY] * len(after), out_specs=VMEM,...  7.09 us
    pallas_call x20, Pallas kernels, product(): pl.pallas_call(body, in_specs=specs, out_specs=out_specs, scratch_shapes=...  5.74 us
  transfers between devices with their start and end apart: 40, of which 22 were waited for; matrix products, arithmetic and copies ran while one was open for 0% of the time, Pallas kernels for 9%

profile of v3, /device:TPU:0, one launch (start us, length us, event | category | flops | bytes accessed | tf_op | source)
XLA Modules:
  0.0 158.5 jit_solution(15638331388533875845)
XLA Ops:
  0.6 1.5 shard_map.95
  2.1 3.0 %collective-permute-start.1 = (bf16[64,2048]{1,0:T(8,128)(2,1)S(1)}, bf16[64,2048]{1,0:T(8,128)(2,1)S(1)}, u32[]{:S(2)}, u32[]{:S(2)}) collective-permute-start(bf16[64,2048]{1,0:T(8,128)(2,1)S(1)} %get-tuple-element.26), channel_id=1, source_target_pairs={{0,4},{1,0},{2,6},{3,2},{4,5},{5,1},{6,7},{7,3},{8,12},{9,8},{10,1... | collective-permute-start | bytes 786440 | tf_op jit(solution)/shard_map/ppermute | solution.py:397
  5.1 0.7 collective-permute-start
  5.8 5.7 %collective-permute-done.1.refs_1_ = bf16[64,2048]{1,0:T(8,128)(2,1)S(1)} collective-permute-done((bf16[64,2048]{1,0:T(8,128)(2,1)S(1)}, bf16[64,2048]{1,0:T(8,128)(2,1)S(1)}, u32[]{:S(2)}, u32[]{:S(2)}) %collective-permute-start.1) | collective-permute-done | bytes 262176 | tf_op jit(solution)/shard_map/ppermute | solution.py:397
  11.6 0.6 collective-permute-start.2
  12.1 3.5 %shard_map.97.refs_1_ = bf16[2048,2048]{1,0:T(8,128)(2,1)S(1)} custom-call(bf16[2048,4096]{1,0:T(8,128)(2,1)} %weight_ref.3), custom_call_target="tpu_custom_call" | custom-call | tf_op jit(solution)/shard_map/pallas_call | solution.py:62
  15.7 3.5 %shard_map.99.refs_1_ = bf16[2048,2048]{1,0:T(8,128)(2,1)S(1)} custom-call(bf16[2048,4096]{1,0:T(8,128)(2,1)} %weight_ref.3), custom_call_target="tpu_custom_call" | custom-call | tf_op jit(solution)/shard_map/pallas_call | solution.py:62
  19.4 4.6 %collective-permute-start.5 = (bf16[64,1024]{1,0:T(8,128)(2,1)S(1)}, bf16[64,1024]{1,0:T(8,128)(2,1)S(1)}, u32[]{:S(2)}, u32[]{:S(2)}) collective-permute-start(bf16[64,1024]{1,0:T(8,128)(2,1)S(1)} %get-tuple-element.31), channel_id=1, source_target_pairs={{0,1},{1,0},{2,3},{3,2},{4,5},{5,4},{6,7},{7,6},{8,9},{9,8},{10,11... | collective-permute-start | bytes 393224 | tf_op jit(solution)/shard_map/ppermute | solution.py:397
  24.0 3.7 %collective-permute-done.5.refs_1_ = bf16[64,1024]{1,0:T(8,128)(2,1)S(1)} collective-permute-done((bf16[64,1024]{1,0:T(8,128)(2,1)S(1)}, bf16[64,1024]{1,0:T(8,128)(2,1)S(1)}, u32[]{:S(2)}, u32[]{:S(2)}) %collective-permute-start.5) | collective-permute-done | bytes 131104 | tf_op jit(solution)/shard_map/ppermute | solution.py:397
  27.7 0.7 collective-permute-start.8
  28.4 0.1 shard_map.108.refs_0_
  28.5 3.0 %collective-permute-start.9 = (bf16[64,1024]{1,0:T(8,128)(2,1)S(1)}, bf16[64,1024]{1,0:T(8,128)(2,1)S(1)}, u32[]{:S(2)}, u32[]{:S(2)}) collective-permute-start(bf16[64,1024]{1,0:T(8,128)(2,1)S(1)} %shard_map.108.refs_0_), channel_id=1, source_target_pairs={{0,4},{1,5},{2,6},{3,7},{4,0},{5,1},{6,2},{7,3},{8,12},{9,13},{10,... | collective-permute-start | bytes 393224 | tf_op jit(solution)/shard_map/ppermute | solution.py:397
  31.5 0.3 collective-permute-start.4
  31.8 2.7 %collective-permute-done.9.refs_1_ = bf16[64,1024]{1,0:T(8,128)(2,1)S(1)} collective-permute-done((bf16[64,1024]{1,0:T(8,128)(2,1)S(1)}, bf16[64,1024]{1,0:T(8,128)(2,1)S(1)}, u32[]{:S(2)}, u32[]{:S(2)}) %collective-permute-start.9) | collective-permute-done | bytes 131104 | tf_op jit(solution)/shard_map/ppermute | solution.py:397
  34.5 1.9 %collective-permute-done.4.refs_1_ = bf16[64,1024]{1,0:T(8,128)(2,1)S(1)} collective-permute-done((bf16[64,1024]{1,0:T(8,128)(2,1)S(1)}, bf16[64,1024]{1,0:T(8,128)(2,1)S(1)}, u32[]{:S(2)}, u32[]{:S(2)}) %collective-permute-start.4) | collective-permute-done | bytes 131104 | tf_op jit(solution)/shard_map/ppermute | solution.py:397
  36.5 0.7 collective-permute-start.6
  37.3 0.2 collective-permute-start.7
  37.5 4.8 %collective-permute-done.7.refs_1_ = bf16[64,1024]{1,0:T(8,128)(2,1)S(1)} collective-permute-done((bf16[64,1024]{1,0:T(8,128)(2,1)S(1)}, bf16[64,1024]{1,0:T(8,128)(2,1)S(1)}, u32[]{:S(2)}, u32[]{:S(2)}) %collective-permute-start.7) | collective-permute-done | bytes 131104 | tf_op jit(solution)/shard_map/ppermute | solution.py:397
  42.5 0.3 shard_map.114
  42.8 0.5 collective-permute-start.12
  43.3 0.7 collective-permute-start.14
  44.0 0.2 collective-permute-done.12
  44.3 0.4 collective-permute-start.15
  44.6 5.5 %collective-permute-done.15.refs_1_ = bf16[64,1024]{1,0:T(8,128)(2,1)S(1)} collective-permute-done((bf16[64,1024]{1,0:T(8,128)(2,1)S(1)}, bf16[64,1024]{1,0:T(8,128)(2,1)S(1)}, u32[]{:S(2)}, u32[]{:S(2)}) %collective-permute-start.15) | collective-permute-done | bytes 131104 | tf_op jit(solution)/shard_map/ppermute | solution.py:397
  50.2 0.7 collective-permute-start.18
  50.9 1.1 collective-permute-start.19
  52.0 0.3 collective-permute-start.13
  52.3 3.6 %collective-permute-done.19.refs_1_ = bf16[64,1024]{1,0:T(8,128)(2,1)S(1)} collective-permute-done((bf16[64,1024]{1,0:T(8,128)(2,1)S(1)}, bf16[64,1024]{1,0:T(8,128)(2,1)S(1)}, u32[]{:S(2)}, u32[]{:S(2)}) %collective-permute-start.19) | collective-permute-done | bytes 131104 | tf_op jit(solution)/shard_map/ppermute | solution.py:397
  56.1 0.9 collective-permute-done.13.refs_1_
  57.1 0.7 collective-permute-start.16
  57.8 1.1 collective-permute-start.17
  58.9 4.0 %collective-permute-done.17.refs_1_ = bf16[64,1024]{1,0:T(8,128)(2,1)S(1)} collective-permute-done((bf16[64,1024]{1,0:T(8,128)(2,1)S(1)}, bf16[64,1024]{1,0:T(8,128)(2,1)S(1)}, u32[]{:S(2)}, u32[]{:S(2)}) %collective-permute-start.17) | collective-permute-done | bytes 131104 | tf_op jit(solution)/shard_map/ppermute | solution.py:397
  63.0 1.1 collective-permute-start.22
  64.1 0.7 collective-permute-start.24
  64.8 2.7 %collective-permute-done.22 = f32[64,256]{1,0:T(8,128)S(1)} collective-permute-done((f32[64,256]{1,0:T(8,128)S(1)}, f32[64,256]{1,0:T(8,128)S(1)}, u32[]{:S(2)}, u32[]{:S(2)}) %collective-permute-start.22) | collective-permute-done | bytes 65568 | tf_op jit(solution)/shard_map/ppermute | solution.py:397
  67.6 0.4 collective-permute-start.25
  67.9 4.7 %collective-permute-done.25.refs_1_ = bf16[64,1024]{1,0:T(8,128)(2,1)S(1)} collective-permute-done((bf16[64,1024]{1,0:T(8,128)(2,1)S(1)}, bf16[64,1024]{1,0:T(8,128)(2,1)S(1)}, u32[]{:S(2)}, u32[]{:S(2)}) %collective-permute-start.25) | collective-permute-done | bytes 131104 | tf_op jit(solution)/shard_map/ppermute | solution.py:397
  72.6 1.3 collective-permute-start.28
  73.9 42.3 %collective-permute-done.28.grad_ref = bf16[64,1024]{1,0:T(8,128)(2,1)S(1)} collective-permute-done((bf16[64,1024]{1,0:T(8,128)(2,1)S(1)}, bf16[64,1024]{1,0:T(8,128)(2,1)S(1)}, u32[]{:S(2)}, u32[]{:S(2)}) %collective-permute-start.28) | collective-permute-done | bytes 131104 | tf_op jit(solution)/shard_map/ppermute | solution.py:397
  116.3 1.3 collective-permute-start.29
  117.6 1.2 collective-permute-start.23
  118.8 2.5 %collective-permute-done.29.refs_1_ = bf16[64,1024]{1,0:T(8,128)(2,1)S(1)} collective-permute-done((bf16[64,1024]{1,0:T(8,128)(2,1)S(1)}, bf16[64,1024]{1,0:T(8,128)(2,1)S(1)}, u32[]{:S(2)}, u32[]{:S(2)}) %collective-permute-start.29) | collective-permute-done | bytes 131104 | tf_op jit(solution)/shard_map/ppermute | solution.py:397
  121.4 1.1 collective-permute-done.23.refs_1_
  122.6 1.3 collective-permute-start.26
  123.9 5.6 %collective-permute-done.26.grad_ref = bf16[64,1024]{1,0:T(8,128)(2,1)S(1)} collective-permute-done((bf16[64,1024]{1,0:T(8,128)(2,1)S(1)}, bf16[64,1024]{1,0:T(8,128)(2,1)S(1)}, u32[]{:S(2)}, u32[]{:S(2)}) %collective-permute-start.26) | collective-permute-done | bytes 131104 | tf_op jit(solution)/shard_map/ppermute | solution.py:397
  129.6 3.0 %collective-permute-start.27 = (bf16[64,1024]{1,0:T(8,128)(2,1)S(1)}, bf16[64,1024]{1,0:T(8,128)(2,1)S(1)}, u32[]{:S(2)}, u32[]{:S(2)}) collective-permute-start(bf16[64,1024]{1,0:T(8,128)(2,1)S(1)} %shard_map.130.refs_0_), channel_id=1, source_target_pairs={{0,4},{1,5},{2,6},{3,7},{4,0},{5,1},{6,2},{7,3},{8,12},{9,13},{10,... | collective-permute-start | bytes 393224 | tf_op jit(solution)/shard_map/ppermute | solution.py:397
  132.5 1.2 shard_map.133.refs_2_
  133.8 1.3 shard_map.134.refs_2_
  135.0 0.4 collective-permute-done.27.refs_1_
  135.6 1.3 collective-permute-start.34
  136.9 1.3 shard_map.136.refs_2_
  138.2 0.9 shard_map.137
  139.1 0.9 shard_map.138
  140.0 3.2 %collective-permute-start.33 = (bf16[64,1024]{1,0:T(8,128)(2,1)S(1)}, bf16[64,1024]{1,0:T(8,128)(2,1)S(1)}, u32[]{:S(2)}, u32[]{:S(2)}) collective-permute-start(bf16[64,1024]{1,0:T(8,128)(2,1)S(1)} %get-tuple-element.48), channel_id=1, source_target_pairs={{0,1},{1,0},{2,3},{3,2},{4,5},{5,4},{6,7},{7,6},{8,9},{9,8},{10,11... | collective-permute-start | bytes 393224 | tf_op jit(solution)/shard_map/ppermute | solution.py:397
  143.3 2.9 %collective-permute-done.34.refs_3_.refs_4_ = bf16[64,2048]{1,0:T(8,128)(2,1)S(1)} collective-permute-done((bf16[64,2048]{1,0:T(8,128)(2,1)S(1)}, bf16[64,2048]{1,0:T(8,128)(2,1)S(1)}, u32[]{:S(2)}, u32[]{:S(2)}) %collective-permute-start.34) | collective-permute-done | bytes 262176 | tf_op jit(solution)/shard_map/ppermute | solution.py:397
  146.2 0.7 shard_map.139
  146.9 1.1 collective-permute-done.35
  148.1 2.0 %collective-permute-start.36 = (f32[2,16]{1,0:T(2,128)S(1)}, f32[2,16]{1,0:T(2,128)S(1)}, u32[]{:S(2)}, u32[]{:S(2)}) collective-permute-start(f32[2,16]{1,0:T(2,128)S(1)} %add.14), channel_id=1, source_target_pairs={{0,4},{1,5},{2,6},{3,7},{4,0},{5,1},{6,2},{7,3},{8,12},{9,13},{10,... | collective-permute-start | bytes 392 | tf_op jit(solution)/shard_map/ppermute | solution.py:397
  150.1 1.6 collective-permute-done.36
  151.7 1.0 collective-permute-start.38
  152.7 3.4 %collective-permute-start.37 = (f32[2,16]{1,0:T(2,128)S(1)}, f32[2,16]{1,0:T(2,128)S(1)}, u32[]{:S(2)}, u32[]{:S(2)}) collective-permute-start(f32[2,16]{1,0:T(2,128)S(1)} %add.15.refs_8_), channel_id=1, source_target_pairs={{0,8},{1,9},{2,10},{3,11},{4,12},{5,13},{6,14},{7,15},{8,0},{9,1},... | collective-permute-start | bytes 392 | tf_op jit(solution)/shard_map/ppermute | solution.py:397
  156.1 1.0 collective-permute-done.39.refs_11_
  157.0 0.6 collective-permute-done.37.refs_9_
  157.6 0.8 shard_map.140
  (76 shorter events, 1.8 us)
Async XLA Ops:
  2.1 9.4 %collective-permute-start.1 = (bf16[64,2048]{1,0:T(8,128)(2,1)S(1)}, bf16[64,2048]{1,0:T(8,128)(2,1)S(1)}, u32[]{:S(2)}, u32[]{:S(2)}) collective-permute-start(bf16[64,2048]{1,0:T(8,128)(2,1)S(1)} %get-tuple-element.26), channel_id=1, source_target_pairs={{0,4},{1,0},{2,6},{3,2},{4,5},{5,1},{6,7},{7,3},{8,12},{9,8},{10,1... | collective-permute-start | bytes 786440 | tf_op jit(solution)/shard_map/ppermute | solution.py:397
  5.1 6.3 %collective-permute-start = (bf16[64,2048]{1,0:T(8,128)(2,1)S(1)}, bf16[64,2048]{1,0:T(8,128)(2,1)S(1)}, u32[]{:S(2)}, u32[]{:S(2)}) collective-permute-start(bf16[64,2048]{1,0:T(8,128)(2,1)S(1)} %get-tuple-element.26), channel_id=1, source_target_pairs={{0,0},{1,4},{2,2},{3,6},{4,1},{5,5},{6,3},{7,7},{8,8},{9,12},{10,1... | collective-permute-start | bytes 786440 | tf_op jit(solution)/shard_map/ppermute | solution.py:397
  11.5 7.8 %collective-permute-start.3 = (bf16[128,1024]{1,0:T(8,128)(2,1)S(1)}, bf16[128,1024]{1,0:T(8,128)(2,1)S(1)}, u32[]{:S(2)}, u32[]{:S(2)}) collective-permute-start(bf16[128,1024]{1,0:T(8,128)(2,1)S(1)} %shard_map.98.refs_0_), channel_id=1, source_target_pairs={{0,2},{1,3},{2,0},{3,1},{4,6},{5,7},{6,4},{7,5},{8,10},{9,11},{10,... | collective-permute-start | bytes 786440 | tf_op jit(solution)/shard_map/ppermute | solution.py:397
  11.6 7.8 %collective-permute-start.2 = (bf16[128,1024]{1,0:T(8,128)(2,1)S(1)}, bf16[128,1024]{1,0:T(8,128)(2,1)S(1)}, u32[]{:S(2)}, u32[]{:S(2)}) collective-permute-start(bf16[128,1024]{1,0:T(8,128)(2,1)S(1)} %shard_map.96.refs_0_), channel_id=1, source_target_pairs={{0,2},{1,3},{2,0},{3,1},{4,6},{5,7},{6,4},{7,5},{8,10},{9,11},{10,... | collective-permute-start | bytes 786440 | tf_op jit(solution)/shard_map/ppermute | solution.py:397
  19.4 8.3 %collective-permute-start.5 = (bf16[64,1024]{1,0:T(8,128)(2,1)S(1)}, bf16[64,1024]{1,0:T(8,128)(2,1)S(1)}, u32[]{:S(2)}, u32[]{:S(2)}) collective-permute-start(bf16[64,1024]{1,0:T(8,128)(2,1)S(1)} %get-tuple-element.31), channel_id=1, source_target_pairs={{0,1},{1,0},{2,3},{3,2},{4,5},{5,4},{6,7},{7,6},{8,9},{9,8},{10,11... | collective-permute-start | bytes 393224 | tf_op jit(solution)/shard_map/ppermute | solution.py:397
  27.7 0.7 collective-permute-start.8
  28.5 5.9 %collective-permute-start.9 = (bf16[64,1024]{1,0:T(8,128)(2,1)S(1)}, bf16[64,1024]{1,0:T(8,128)(2,1)S(1)}, u32[]{:S(2)}, u32[]{:S(2)}) collective-permute-start(bf16[64,1024]{1,0:T(8,128)(2,1)S(1)} %shard_map.108.refs_0_), channel_id=1, source_target_pairs={{0,4},{1,5},{2,6},{3,7},{4,0},{5,1},{6,2},{7,3},{8,12},{9,13},{10,... | collective-permute-start | bytes 393224 | tf_op jit(solution)/shard_map/ppermute | solution.py:397
  31.5 5.0 %collective-permute-start.4 = (bf16[64,1024]{1,0:T(8,128)(2,1)S(1)}, bf16[64,1024]{1,0:T(8,128)(2,1)S(1)}, u32[]{:S(2)}, u32[]{:S(2)}) collective-permute-start(bf16[64,1024]{1,0:T(8,128)(2,1)S(1)} %get-tuple-element.29), channel_id=1, source_target_pairs={{0,1},{1,0},{2,3},{3,2},{4,5},{5,4},{6,7},{7,6},{8,9},{9,8},{10,11... | collective-permute-start | bytes 393224 | tf_op jit(solution)/shard_map/ppermute | solution.py:397
  34.5 3.0 %collective-permute-start.10 = (bf16[128,1024]{1,0:T(8,128)(2,1)S(1)}, bf16[128,1024]{1,0:T(8,128)(2,1)S(1)}, u32[]{:S(2)}, u32[]{:S(2)}) collective-permute-start(bf16[128,1024]{1,0:T(8,128)(2,1)S(1)} %shard_map.109.refs_0_), channel_id=1, source_target_pairs={{0,2},{1,3},{2,0},{3,1},{4,6},{5,7},{6,4},{7,5},{8,10},{9,11},{10,... | collective-permute-start | bytes 786440 | tf_op jit(solution)/shard_map/ppermute | solution.py:397
  36.5 0.7 collective-permute-start.6
  37.3 5.0 %collective-permute-start.7 = (bf16[64,1024]{1,0:T(8,128)(2,1)S(1)}, bf16[64,1024]{1,0:T(8,128)(2,1)S(1)}, u32[]{:S(2)}, u32[]{:S(2)}) collective-permute-start(bf16[64,1024]{1,0:T(8,128)(2,1)S(1)} %shard_map.107.refs_0_), channel_id=1, source_target_pairs={{0,4},{1,5},{2,6},{3,7},{4,0},{5,1},{6,2},{7,3},{8,12},{9,13},{10,... | collective-permute-start | bytes 393224 | tf_op jit(solution)/shard_map/ppermute | solution.py:397
  37.5 5.0 %copy-start.1 = (bf16[2048,256]{1,0:T(8,128)(2,1)S(1)}, bf16[2048,256]{1,0:T(8,128)(2,1)}, u32[]{:S(2)}) copy-start(bf16[2048,256]{1,0:T(8,128)(2,1)} %factor_ref.1) | copy-start | bytes 3145732
  37.5 5.0 %copy-start.3 = (bf16[64,2048]{1,0:T(8,128)(2,1)S(1)}, bf16[64,2048]{1,0:T(8,128)(2,1)}, u32[]{:S(2)}) copy-start(bf16[64,2048]{1,0:T(8,128)(2,1)} %value_ref.1) | copy-start | bytes 786436
  42.4 1.9 %collective-permute-start.11 = (bf16[128,1024]{1,0:T(8,128)(2,1)S(1)}, bf16[128,1024]{1,0:T(8,128)(2,1)S(1)}, u32[]{:S(2)}, u32[]{:S(2)}) collective-permute-start(bf16[128,1024]{1,0:T(8,128)(2,1)S(1)} %shard_map.112.refs_0_), channel_id=1, source_target_pairs={{0,2},{1,3},{2,0},{3,1},{4,6},{5,7},{6,4},{7,5},{8,10},{9,11},{10,... | collective-permute-start | bytes 786440 | tf_op jit(solution)/shard_map/ppermute | solution.py:397
  42.8 1.4 collective-permute-start.12
  43.3 1.3 collective-permute-start.14
  44.3 5.8 %collective-permute-start.15 = (bf16[64,1024]{1,0:T(8,128)(2,1)S(1)}, bf16[64,1024]{1,0:T(8,128)(2,1)S(1)}, u32[]{:S(2)}, u32[]{:S(2)}) collective-permute-start(bf16[64,1024]{1,0:T(8,128)(2,1)S(1)} %get-tuple-element.37), channel_id=1, source_target_pairs={{0,1},{1,0},{2,3},{3,2},{4,5},{5,4},{6,7},{7,6},{8,9},{9,8},{10,11... | collective-permute-start | bytes 393224 | tf_op jit(solution)/shard_map/ppermute | solution.py:397
  50.2 0.7 collective-permute-start.18
  50.9 5.0 %collective-permute-start.19 = (bf16[64,1024]{1,0:T(8,128)(2,1)S(1)}, bf16[64,1024]{1,0:T(8,128)(2,1)S(1)}, u32[]{:S(2)}, u32[]{:S(2)}) collective-permute-start(bf16[64,1024]{1,0:T(8,128)(2,1)S(1)} %shard_map.120.refs_0_), channel_id=1, source_target_pairs={{0,4},{1,5},{2,6},{3,7},{4,0},{5,1},{6,2},{7,3},{8,12},{9,13},{10,... | collective-permute-start | bytes 393224 | tf_op jit(solution)/shard_map/ppermute | solution.py:397
  52.0 5.0 %collective-permute-start.13 = (bf16[64,1024]{1,0:T(8,128)(2,1)S(1)}, bf16[64,1024]{1,0:T(8,128)(2,1)S(1)}, u32[]{:S(2)}, u32[]{:S(2)}) collective-permute-start(bf16[64,1024]{1,0:T(8,128)(2,1)S(1)} %get-tuple-element.35), channel_id=1, source_target_pairs={{0,1},{1,0},{2,3},{3,2},{4,5},{5,4},{6,7},{7,6},{8,9},{9,8},{10,11... | collective-permute-start | bytes 393224 | tf_op jit(solution)/shard_map/ppermute | solution.py:397
  56.0 2.9 %collective-permute-start.20 = (bf16[128,1024]{1,0:T(8,128)(2,1)S(1)}, bf16[128,1024]{1,0:T(8,128)(2,1)S(1)}, u32[]{:S(2)}, u32[]{:S(2)}) collective-permute-start(bf16[128,1024]{1,0:T(8,128)(2,1)S(1)} %shard_map.121.refs_0_), channel_id=1, source_target_pairs={{0,2},{1,3},{2,0},{3,1},{4,6},{5,7},{6,4},{7,5},{8,10},{9,11},{10,... | collective-permute-start | bytes 786440 | tf_op jit(solution)/shard_map/ppermute | solution.py:397
  57.1 0.7 collective-permute-start.16
  57.8 5.0 %collective-permute-start.17 = (bf16[64,1024]{1,0:T(8,128)(2,1)S(1)}, bf16[64,1024]{1,0:T(8,128)(2,1)S(1)}, u32[]{:S(2)}, u32[]{:S(2)}) collective-permute-start(bf16[64,1024]{1,0:T(8,128)(2,1)S(1)} %shard_map.119.refs_0_), channel_id=1, source_target_pairs={{0,4},{1,5},{2,6},{3,7},{4,0},{5,1},{6,2},{7,3},{8,12},{9,13},{10,... | collective-permute-start | bytes 393224 | tf_op jit(solution)/shard_map/ppermute | solution.py:397
  62.9 4.6 %collective-permute-start.21 = (bf16[128,1024]{1,0:T(8,128)(2,1)S(1)}, bf16[128,1024]{1,0:T(8,128)(2,1)S(1)}, u32[]{:S(2)}, u32[]{:S(2)}) collective-permute-start(bf16[128,1024]{1,0:T(8,128)(2,1)S(1)} %shard_map.124.refs_0_), channel_id=1, source_target_pairs={{0,2},{1,3},{2,0},{3,1},{4,6},{5,7},{6,4},{7,5},{8,10},{9,11},{10,... | collective-permute-start | bytes 786440 | tf_op jit(solution)/shard_map/ppermute | solution.py:397
  63.0 4.5 %collective-permute-start.22 = (f32[64,256]{1,0:T(8,128)S(1)}, f32[64,256]{1,0:T(8,128)S(1)}, u32[]{:S(2)}, u32[]{:S(2)}) collective-permute-start(f32[64,256]{1,0:T(8,128)S(1)} %add.12.refs_3_), channel_id=1, source_target_pairs={{0,4},{1,5},{2,6},{3,7},{4,0},{5,1},{6,2},{7,3},{8,12},{9,13},{10,... | collective-permute-start | bytes 196616 | tf_op jit(solution)/shard_map/ppermute | solution.py:397
  64.1 3.8 %collective-permute-start.24 = (bf16[64,2048]{1,0:T(8,128)(2,1)S(1)}, bf16[64,2048]{1,0:T(8,128)(2,1)S(1)}, u32[]{:S(2)}, u32[]{:S(2)}) collective-permute-start(bf16[64,2048]{1,0:T(8,128)(2,1)S(1)} %get-tuple-element.42.refs_6_), channel_id=1, source_target_pairs={{16,8},{17,9},{18,10},{19,11},{20,12},{21,13},{22,14},{23,15}} | collective-permute-start | bytes 786440 | tf_op jit(solution)/shard_map/ppermute | solution.py:397
  67.6 5.0 %collective-permute-start.25 = (bf16[64,1024]{1,0:T(8,128)(2,1)S(1)}, bf16[64,1024]{1,0:T(8,128)(2,1)S(1)}, u32[]{:S(2)}, u32[]{:S(2)}) collective-permute-start(bf16[64,1024]{1,0:T(8,128)(2,1)S(1)} %get-tuple-element.43), channel_id=1, source_target_pairs={{0,1},{1,0},{2,3},{3,2},{4,5},{5,4},{6,7},{7,6},{8,9},{9,8},{10,11... | collective-permute-start | bytes 393224 | tf_op jit(solution)/shard_map/ppermute | solution.py:397
  72.6 43.6 %collective-permute-start.28 = (bf16[64,1024]{1,0:T(8,128)(2,1)S(1)}, bf16[64,1024]{1,0:T(8,128)(2,1)S(1)}, u32[]{:S(2)}, u32[]{:S(2)}) collective-permute-start(bf16[64,1024]{1,0:T(8,128)(2,1)S(1)} %shard_map.128.refs_3_), channel_id=1, source_target_pairs={{8,0},{9,4},{10,2},{11,6},{12,1},{13,5},{14,3},{15,7}} | collective-permute-start | bytes 393224 | tf_op jit(solution)/shard_map/ppermute | solution.py:397
  116.3 5.0 %collective-permute-start.29 = (bf16[64,1024]{1,0:T(8,128)(2,1)S(1)}, bf16[64,1024]{1,0:T(8,128)(2,1)S(1)}, u32[]{:S(2)}, u32[]{:S(2)}) collective-permute-start(bf16[64,1024]{1,0:T(8,128)(2,1)S(1)} %shard_map.131.refs_0_), channel_id=1, source_target_pairs={{0,4},{1,5},{2,6},{3,7},{4,0},{5,1},{6,2},{7,3},{8,12},{9,13},{10,... | collective-permute-start | bytes 393224 | tf_op jit(solution)/shard_map/ppermute | solution.py:397
  117.6 5.0 %collective-permute-start.23 = (bf16[64,1024]{1,0:T(8,128)(2,1)S(1)}, bf16[64,1024]{1,0:T(8,128)(2,1)S(1)}, u32[]{:S(2)}, u32[]{:S(2)}) collective-permute-start(bf16[64,1024]{1,0:T(8,128)(2,1)S(1)} %get-tuple-element.41), channel_id=1, source_target_pairs={{0,1},{1,0},{2,3},{3,2},{4,5},{5,4},{6,7},{7,6},{8,9},{9,8},{10,11... | collective-permute-start | bytes 393224 | tf_op jit(solution)/shard_map/ppermute | solution.py:397
  121.3 12.4 %collective-permute-start.30 = (bf16[128,1024]{1,0:T(8,128)(2,1)S(1)}, bf16[128,1024]{1,0:T(8,128)(2,1)S(1)}, u32[]{:S(2)}, u32[]{:S(2)}) collective-permute-start(bf16[128,1024]{1,0:T(8,128)(2,1)S(1)} %shard_map.132.refs_0_), channel_id=1, source_target_pairs={{0,2},{1,3},{2,0},{3,1},{4,6},{5,7},{6,4},{7,5},{8,10},{9,11},{10,... | collective-permute-start | bytes 786440 | tf_op jit(solution)/shard_map/ppermute | solution.py:397
  122.6 6.9 %collective-permute-start.26 = (bf16[64,1024]{1,0:T(8,128)(2,1)S(1)}, bf16[64,1024]{1,0:T(8,128)(2,1)S(1)}, u32[]{:S(2)}, u32[]{:S(2)}) collective-permute-start(bf16[64,1024]{1,0:T(8,128)(2,1)S(1)} %get-tuple-element.44), channel_id=1, source_target_pairs={{8,0},{9,4},{10,2},{11,6},{12,1},{13,5},{14,3},{15,7}} | collective-permute-start | bytes 393224 | tf_op jit(solution)/shard_map/ppermute | solution.py:397
  129.6 5.9 %collective-permute-start.27 = (bf16[64,1024]{1,0:T(8,128)(2,1)S(1)}, bf16[64,1024]{1,0:T(8,128)(2,1)S(1)}, u32[]{:S(2)}, u32[]{:S(2)}) collective-permute-start(bf16[64,1024]{1,0:T(8,128)(2,1)S(1)} %shard_map.130.refs_0_), channel_id=1, source_target_pairs={{0,4},{1,5},{2,6},{3,7},{4,0},{5,1},{6,2},{7,3},{8,12},{9,13},{10,... | collective-permute-start | bytes 393224 | tf_op jit(solution)/shard_map/ppermute | solution.py:397
  135.5 2.7 %collective-permute-start.31 = (bf16[128,1024]{1,0:T(8,128)(2,1)S(1)}, bf16[128,1024]{1,0:T(8,128)(2,1)S(1)}, u32[]{:S(2)}, u32[]{:S(2)}) collective-permute-start(bf16[128,1024]{1,0:T(8,128)(2,1)S(1)} %shard_map.135.refs_0_), channel_id=1, source_target_pairs={{0,2},{1,3},{2,0},{3,1},{4,6},{5,7},{6,4},{7,5},{8,10},{9,11},{10,... | collective-permute-start | bytes 786440 | tf_op jit(solution)/shard_map/ppermute | solution.py:397
  135.6 10.6 %collective-permute-start.34 = (bf16[64,2048]{1,0:T(8,128)(2,1)S(1)}, bf16[64,2048]{1,0:T(8,128)(2,1)S(1)}, u32[]{:S(2)}, u32[]{:S(2)}) collective-permute-start(bf16[64,2048]{1,0:T(8,128)(2,1)S(1)} %get-tuple-element.49.refs_7_), channel_id=1, source_target_pairs={{8,0},{9,1},{10,2},{11,3},{12,4},{13,5},{14,6},{15,7}} | collective-permute-start | bytes 786440 | tf_op jit(solution)/shard_map/ppermute | solution.py:397
  138.1 8.0 %copy-start = (bf16[2048,256]{1,0:T(8,128)(2,1)S(1)}, bf16[2048,256]{1,0:T(8,128)(2,1)}, u32[]{:S(2)}) copy-start(bf16[2048,256]{1,0:T(8,128)(2,1)} %refs_4_.1) | copy-start | bytes 3145732
  138.2 8.0 %copy-start.2 = (bf16[64,2048]{1,0:T(8,128)(2,1)S(1)}, bf16[64,2048]{1,0:T(8,128)(2,1)}, u32[]{:S(2)}) copy-start(bf16[64,2048]{1,0:T(8,128)(2,1)} %preact_ref.3) | copy-start | bytes 786436
  138.2 8.0 %copy-start.4 = (s32[64]{0:T(128)S(1)}, s32[64]{0:T(128)}, u32[]{:S(2)}) copy-start(s32[64]{0:T(128)} %param.10) | copy-start | bytes 772
  140.0 17.6 %collective-permute-start.33 = (bf16[64,1024]{1,0:T(8,128)(2,1)S(1)}, bf16[64,1024]{1,0:T(8,128)(2,1)S(1)}, u32[]{:S(2)}, u32[]{:S(2)}) collective-permute-start(bf16[64,1024]{1,0:T(8,128)(2,1)S(1)} %get-tuple-element.48), channel_id=1, source_target_pairs={{0,1},{1,0},{2,3},{3,2},{4,5},{5,4},{6,7},{7,6},{8,9},{9,8},{10,11... | collective-permute-start | bytes 393224 | tf_op jit(solution)/shard_map/ppermute | solution.py:397
  143.2 14.4 %collective-permute-start.32 = (bf16[64,1024]{1,0:T(8,128)(2,1)S(1)}, bf16[64,1024]{1,0:T(8,128)(2,1)S(1)}, u32[]{:S(2)}, u32[]{:S(2)}) collective-permute-start(bf16[64,1024]{1,0:T(8,128)(2,1)S(1)} %get-tuple-element.47), channel_id=1, source_target_pairs={{0,1},{1,0},{2,3},{3,2},{4,5},{5,4},{6,7},{7,6},{8,9},{9,8},{10,11... | collective-permute-start | bytes 393224 | tf_op jit(solution)/shard_map/ppermute | solution.py:397
  146.9 1.2 collective-permute-start.35
  148.1 3.6 %collective-permute-start.36 = (f32[2,16]{1,0:T(2,128)S(1)}, f32[2,16]{1,0:T(2,128)S(1)}, u32[]{:S(2)}, u32[]{:S(2)}) collective-permute-start(f32[2,16]{1,0:T(2,128)S(1)} %add.14), channel_id=1, source_target_pairs={{0,4},{1,5},{2,6},{3,7},{4,0},{5,1},{6,2},{7,3},{8,12},{9,13},{10,... | collective-permute-start | bytes 392 | tf_op jit(solution)/shard_map/ppermute | solution.py:397
  151.7 5.4 %collective-permute-start.39 = (f32[2,16]{1,0:T(2,128)S(1)}, f32[2,16]{1,0:T(2,128)S(1)}, u32[]{:S(2)}, u32[]{:S(2)}) collective-permute-start(f32[2,16]{1,0:T(2,128)S(1)} %add.15.refs_8_), channel_id=1, source_target_pairs={{0,24},{1,25},{2,26},{3,27},{4,28},{5,29},{6,30},{7,31},{8,16},{9,... | collective-permute-start | bytes 392 | tf_op jit(solution)/shard_map/ppermute | solution.py:397
  151.7 5.4 %collective-permute-start.38 = (f32[2,16]{1,0:T(2,128)S(1)}, f32[2,16]{1,0:T(2,128)S(1)}, u32[]{:S(2)}, u32[]{:S(2)}) collective-permute-start(f32[2,16]{1,0:T(2,128)S(1)} %add.15.refs_8_), channel_id=1, source_target_pairs={{0,16},{1,17},{2,18},{3,19},{4,20},{5,21},{6,22},{7,23},{8,24},{9,... | collective-permute-start | bytes 392 | tf_op jit(solution)/shard_map/ppermute | solution.py:397
  152.7 4.9 %collective-permute-start.37 = (f32[2,16]{1,0:T(2,128)S(1)}, f32[2,16]{1,0:T(2,128)S(1)}, u32[]{:S(2)}, u32[]{:S(2)}) collective-permute-start(f32[2,16]{1,0:T(2,128)S(1)} %add.15.refs_8_), channel_id=1, source_target_pairs={{0,8},{1,9},{2,10},{3,11},{4,12},{5,13},{6,14},{7,15},{8,0},{9,1},... | collective-permute-start | bytes 392 | tf_op jit(solution)/shard_map/ppermute | solution.py:397
